TPU v7x, 512 devices: a whole 4x8x8 slice. The times are simulated.
512 devices in a mesh: win: 16 (over x_hi, y), lat: 32 (over z, x_lo, core).
Axes of the slice: x: 4 (x_hi: 2, x_lo: 2; x = x_hi * 2 + x_lo), y: 8, z: 8, core: 2. Of those that a mesh axis runs over, the one named last changes fastest.
Arguments:
- state: float32 [16, 1, 1024, 2048], P('win', None, 'lat'), may hold values from -6 to 6
- multipliers: float32 [16, 1, 1024, 2048], P('win', None, 'lat'), may hold values from -3 to 3
- observations: float32 [16, 2, 1, 1024, 2048], P('win', None, None, 'lat'), may hold values from -6 to 6
- obs_mask: int32 [16, 2, 1024, 2048], P('win', None, 'lat'), may hold values 0 or 1
- speed: float32 [1], replicated, may hold values from 0.1 to 0.3
- drift: float32 [1], replicated, may hold values from 0.1 to 0.4
- kappa: float32 [1], replicated, may hold values from 0.05 to 0.2
- lat_spectrum: float32 [1, 1024], replicated, may hold values from 0.05 to 1
- lon_spectrum: float32 [1, 2048], replicated, may hold values from 0.05 to 1
Outputs:
- new_state: float32 [16, 1, 1024, 2048], P('win', None, 'lat')
- new_multipliers: float32 [16, 1, 1024, 2048], P('win', None, 'lat')
All inputs are finite; a program needn't handle non-finite values. No bound on the sum of `obs_mask` on one device may be relied on, other than what follows from the above.
Results may differ from a plain program's by a relative error of at most 0.0001.
Values sent between devices are 32-bit elements; how exact they have to be, the bound alone decides.
A program may use at most 64 MiB of HBM per device.

v0:
```python
import math

import jax
import jax.numpy as jnp
from jax import lax
from jax.sharding import Mesh
from jax.sharding import PartitionSpec as P

LAT = ("lat_0", "lat_1", "lat_2")
WIN = ("win_0", "win_1")


def extended(block, sides, width):
    for axis, dim in sides:
        count = lax.axis_size(axis)
        forward = [(i, i + 1) for i in range(count - 1)]
        backward = [(target, source) for source, target in forward]
        low = lax.ppermute(
            lax.slice_in_dim(block, block.shape[dim] - width, None, axis=dim), axis, forward
        )
        high = lax.ppermute(lax.slice_in_dim(block, 0, width, axis=dim), axis, backward)
        block = jnp.concatenate([low, block, high], axis=dim)
    return block


def passed_along(value, axis, steps):
    count = lax.axis_size(axis)
    first, last = (max(0, -steps), min(count, count - steps))
    return lax.ppermute(value, axis, [(source, source + steps) for source in range(first, last)])


def neutral_like(array, identity):
    return jnp.broadcast_to(jnp.asarray(identity, array.dtype), array.shape)


def entering(array, axes, combine, identity):
    before = start = neutral_like(array, identity)
    running = array
    for axis in reversed(axes):
        peers, here = (lax.axis_size(axis), lax.axis_index(axis))
        pieces = lax.all_gather(running, axis)
        inside, running = (start, start)
        for k in range(peers):
            passed = k < here
            running = combine(running, pieces[k])
            inside = jnp.where(passed, running, inside)
        before = combine(inside, before)
    return before


def in_blocks(array, dim, peers):
    before, after = (array.shape[:dim], array.shape[dim + 1 :])
    return jnp.moveaxis(array.reshape(*before, peers, -1, *after), dim, 0)


def laid_out(tiles, dim):
    tiles = jnp.moveaxis(tiles, 0, dim)
    shape = tiles.shape
    return tiles.reshape(*shape[:dim], shape[dim] * shape[dim + 1], *shape[dim + 2 :])


def moved_by_axis(tiles, axes, turns):
    shape = [lax.axis_size(a) for a in axes]
    tiles = tiles.reshape(*shape, *tiles.shape[1:])
    for k in turns:
        tiles = lax.all_to_all(tiles, axes[k], split_axis=k, concat_axis=k, tiled=True)
    return tiles.reshape(-1, *tiles.shape[len(axes) :])


def core_and_chips(array, groups, turns, split_dim, concat_dim):
    peers = lax.axis_size(groups[0]) * lax.axis_size(groups[1])
    tiles = in_blocks(array, split_dim, peers)
    return laid_out(moved_by_axis(tiles, groups, turns), concat_dim)


def hartley(count):
    index = jnp.arange(count, dtype=jnp.int32)
    product = index[:, None] * index[None, :] % count
    angle = product.astype(jnp.float32) * (2.0 * math.pi / count)
    return jnp.cos(angle) + jnp.sin(angle)


def advance(padded, speed, drift, kappa):
    field = padded[:, 1:-1]
    north = padded[:, 2:]
    south = padded[:, :-2]
    east = jnp.roll(field, -1, axis=-1)
    west = jnp.roll(field, 1, axis=-1)
    speed_c = speed[:, None, None]
    drift_c = drift[:, None, None]
    kappa_c = kappa[:, None, None]
    return (
        field
        - speed_c * field * (east - west) * 0.5
        - drift_c * (north - south) * 0.5
        + kappa_c * (east + west + north + south - 4.0 * field)
    )


def per_device(
    state, multipliers, observations, obs_mask, speed, drift, kappa, lat_spectrum, lon_spectrum
):
    high = lax.Precision.HIGHEST
    field = state[0]
    lam = multipliers[0]
    observed = observations[0]
    mask = obs_mask[0].astype(jnp.float32)
    band = field.shape[1]
    nlon = field.shape[2]
    bands = lax.axis_size(LAT)
    nlat = band * bands
    columns = nlon // bands
    lat_index = lax.axis_index(LAT)
    win_index = lax.axis_index(WIN)
    h_lon = hartley(nlon)
    h_lat = hartley(nlat)
    lon_part = lax.dynamic_slice_in_dim(lon_spectrum, lat_index * columns, columns, 1)
    weight = lat_spectrum[:, :, None] * lon_part[:, None, :]
    divisor = jnp.maximum(win_index, 1).astype(jnp.float32)
    rows_global = lat_index * band + jnp.arange(-1, band + 1, dtype=jnp.int32)
    inside = ((rows_global >= 0) & (rows_global < nlat))[None, :, None]
    padded = extended(field, ((LAT, 1),), 2)
    widened = advance(padded, speed, drift, kappa)
    widened = jnp.where(inside, widened, jnp.float32(0.0))
    first = widened[:, 1:-1]
    second = advance(widened, speed, drift, kappa)
    defect = mask[0][None] * (observed[0] - first) + mask[1][None] * (observed[1] - second)
    prior_end = passed_along(second, WIN, 1)
    mismatch = jnp.where(win_index > 0, field - prior_end, jnp.float32(0.0))
    lam = lam + 0.5 * mismatch
    carried = entering(lam, WIN, lambda earlier, later: earlier + later, jnp.zeros_like(lam))
    resid = defect + lam - carried / divisor
    spectral = jnp.matmul(resid, h_lon, precision=high)
    spectral = core_and_chips(spectral, (("lat_0", "lat_1"), "lat_2"), (1, 0), 2, 1)
    spectral = jnp.einsum("ij,ljk->lik", h_lat, spectral, precision=high) * weight
    spectral = jnp.einsum("ij,ljk->lik", h_lat, spectral, precision=high)
    spectral = lax.all_to_all(spectral, LAT, split_axis=1, concat_axis=2, tiled=True)
    increment = jnp.matmul(spectral, h_lon, precision=high) / (nlat * nlon)
    field = field + 0.5 * increment
    return (field[None], lam[None])


def solution(mesh):
    finer = Mesh(mesh.devices.reshape(2, 8, 8, 2, 2), ("win_0", "win_1", "lat_0", "lat_1", "lat_2"))
    placed = (
        P(WIN, None, LAT, None),
        P(WIN, None, LAT, None),
        P(WIN, None, None, LAT, None),
        P(WIN, None, LAT, None),
        P(),
        P(),
        P(),
        P(),
        P(),
    )
    return jax.shard_map(
        per_device,
        mesh=finer,
        in_specs=placed,
        out_specs=(P(WIN, None, LAT, None), P(WIN, None, LAT, None)),
        check_vma=False,
    )
```

profile of v0, /device:TPU:6, one launch (start us, length us, event | category | flops | bytes accessed | tf_op | source)
XLA Modules:
  0.0 319.1 jit_solution(2308843444080930673)
XLA Ops:
  7.2 0.0 copy-start
  7.2 0.0 copy-start.1
  7.2 0.0 copy-start.4
  7.2 0.0 copy-start.3
  7.2 0.0 all-gather.3.cloned.1.call-start
  7.3 1.0 fusion.102
  8.2 1.9 collective-permute-start
  10.2 3.6 %collective-permute-start.1 = (f32[1,2,2048]{2,1,0:T(2,128)S(1)}, f32[1,2,2048]{2,1,0:T(2,128)S(1)}, u32[]{:S(2)}, u32[]{:S(2)}) collective-permute-start(f32[1,2,2048]{2,1,0:T(2,128)S(1)} %get-tuple-element.10), channel_id=1, source_target_pairs={{1,0},{2,1},{3,2},{4,3},{5,4},{6,5},{7,6},{8,7},{9,8},{10,9},{11,1... | collective-permute-start | bytes 49160 | tf_op jit(solution)/shard_map/ppermute | solution.py:21
  15.8 0.0 collective-permute-done
  15.8 0.0 collective-permute-done.1
  15.8 1.0 pad_maximum_fusion.4
  16.8 0.2 fusion.101
  16.9 1.5 add_select_fusion.3
  18.4 0.1 fusion.99
  18.6 0.1 fusion.100
  18.6 0.2 multiply_add_fusion
  18.9 3.5 %collective-permute-start.2 = (f32[1,32,2048]{2,1,0:T(8,128)S(1)}, f32[1,32,2048]{2,1,0:T(8,128)S(1)}, u32[]{:S(2)}, u32[]{:S(2)}) collective-permute-start(f32[1,32,2048]{2,1,0:T(8,128)S(1)} %multiply_add_fusion), channel_id=1, source_target_pairs={{0,32},{32,64},{64,96},{96,128},{128,160},{160,192},{192,224},{224... | collective-permute-start | bytes 786440 | tf_op jit(solution)/shard_map/ppermute | solution.py:29
  22.4 9.1 %collective-permute-done.2 = f32[1,32,2048]{2,1,0:T(8,128)S(1)} collective-permute-done((f32[1,32,2048]{2,1,0:T(8,128)S(1)}, f32[1,32,2048]{2,1,0:T(8,128)S(1)}, u32[]{:S(2)}, u32[]{:S(2)}) %collective-permute-start.2) | collective-permute-done | bytes 262176 | tf_op jit(solution)/shard_map/ppermute | solution.py:29
  31.5 0.0 copy-done.1
  31.5 0.0 copy-done.4
  31.5 0.7 bitcast_add_fusion
  32.2 0.0 all-gather.3.cloned.1.call-update
  32.3 0.1 mul.274
  32.4 0.0 copy-done.3
  32.4 0.0 copy-start.2
  32.4 0.0 copy-start.5
  32.4 69.5 %sine_add_fusion = f32[2048,2048]{1,0:T(8,128)} fusion(s32[2048]{0:T(1024)S(1)} %mul.274), kind=kLoop, calls=%fused_computation.18 | loop fusion | flops 62914560 | bytes 16785408 | tf_op jit(solution)/shard_map/add | solution.py:80
  102.0 0.0 all-gather.3.cloned.1.call-done
  102.0 1.6 fusion.53
  103.6 10.4 %all_gather.12 = f32[2,1,32,2048]{3,2,1,0:T(8,128)S(1)} all-gather(f32[1,1,32,2048]{3,2,1,0:T(8,128)S(1)} %get-tuple-element.2), channel_id=1, replica_groups=mesh['win_0'=2,'win_1'=8,'lat_0'=8,'lat_1'=2,'lat_2'=2] {'win_0'}, dimensions={0}, use_global_device_ids=true | all-gather | bytes 786432 | tf_op jit(solution)/shard_map/all_gather | solution.py:41
  114.0 0.0 copy-done.2
  114.0 0.0 copy-done.5
  114.0 25.6 %fusion.51 = f32[32,32,64]{2,0,1:T(8,128)S(1)} fusion(f32[32,64,2048]{2,1,0:T(8,128)} %bitcast.111, f32[2,1,32,2048]{3,2,1,0:T(8,128)S(1)} %all_gather.12, f32[1,32,2048]{2,1,0:T(8,128)S(1)} %copy-done.2, f32[1,2,32,2048]{3,2,1,0:T(8,128)S(1)} %convert_element_type.24, f32[1,1,32,2048]{3,2,1,0:T(8,128)S(1)} %get-tuple-element.2, ...), kind=kOutput, calls=%fused_computation.63 | convolution fusion | flops 1612251136 | bytes 21495822 | tf_op jit(solution)/shard_map/dot_general | solution.py:133
  139.6 0.0 copy-start.6
  139.7 0.3 reshape.749
  140.0 4.2 %all_to_all.25 = f32[2,1,32768]{2,1,0:T(1,128)S(1)} all-to-all(f32[2,1,32768]{2,1,0:T(1,128)S(1)} %reshape.749), channel_id=1, replica_groups=mesh['win_0'=2,'win_1'=8,'lat_0'=8,'lat_1'=2,'lat_2'=2] {'lat_2'}, dimensions={0} | all-to-all | bytes 524288 | tf_op jit(solution)/shard_map/all_to_all | solution.py:66
  144.2 0.6 broadcast.377
  144.8 1.5 reduce
  146.3 0.3 reshape.750
  146.7 1.0 reshape.751
  147.7 13.3 %all-to-all-start.1 = ((f32[16,1,4096]{2,1,0:T(1,128)}), f32[16,1,4096]{2,1,0:T(1,128)S(1)}, u32[]{:S(2)}, u32[]{:S(2)}) async-start(f32[16,1,4096]{2,1,0:T(1,128)} %reshape.751), calls=%async_computation.1 | async-start | bytes 524288 | tf_op jit(solution)/shard_map/all_to_all | solution.py:66
  161.0 0.0 copy-done
  161.0 0.1 dynamic-slice_bitcast_fusion
  161.1 10.7 %all-to-all-done.1 = f32[16,1,4096]{2,1,0:T(1,128)S(1)} async-done(((f32[16,1,4096]{2,1,0:T(1,128)}), f32[16,1,4096]{2,1,0:T(1,128)S(1)}, u32[]{:S(2)}, u32[]{:S(2)}) %all-to-all-start.1) | async-done | bytes 262176 | tf_op jit(solution)/shard_map/all_to_all | solution.py:66
  171.8 1.3 reduce.1
  173.1 0.2 reshape.752
  173.4 0.0 copy-done.6
  173.4 20.7 %fusion.42 = f32[1024,64]{0,1:T(8,128)S(1)} fusion(f32[1024,64]{1,0:T(8,128)S(1)} %bitcast.120, f32[64]{0:T(128)S(1)} %dynamic-slice_bitcast_fusion, f32[1024]{0:T(1024)S(1)} %bitcast.121), kind=kOutput, calls=%fused_computation.45 | convolution fusion | flops 821166080 | bytes 528640 | tf_op jit(solution)/shard_map/ij,ljk->lik/dot_general | solution.py:135
  194.1 20.6 %fusion.40 = f32[1,1024,64]{1,2,0:T(8,128)S(1)} fusion(f32[1024,64]{0,1:T(8,128)S(1)} %fusion.42), kind=kOutput, calls=%fused_computation.43 | convolution fusion | flops 821035008 | bytes 524288 | tf_op jit(solution)/shard_map/ij,ljk->lik/dot_general | solution.py:136
  214.7 0.3 copy.15
  215.1 2.0 reduce.2
  217.1 0.3 reshape.753
  217.4 16.3 %all_to_all.26 = f32[32,1,2048]{2,1,0:T(1,128)S(1)} all-to-all(f32[32,1,2048]{2,1,0:T(1,128)S(1)} %reshape.753), channel_id=1, replica_groups=mesh['win_0'=2,'win_1'=8,'lat_0'=8,'lat_1'=2,'lat_2'=2] {'lat_0','lat_1'..., dimensions={0} | all-to-all | bytes 524288 | tf_op jit(solution)/shard_map/all_to_all | solution.py:137
  233.8 1.3 reduce.3
  235.1 0.7 reshape.754
  235.8 0.3 copy.16
  236.1 0.2 reshape.702
  236.3 76.0 %fusion.34 = f32[1,1,32,2048]{3,2,1,0:T(8,128)} fusion(f32[32,2048]{1,0:T(8,128)S(1)} %reshape.702, f32[1,1,32,2048]{3,2,1,0:T(8,128)S(1)} %copy-done.1), kind=kOutput, calls=%fused_computation.39 | convolution fusion | flops 1673658368 | bytes 786432 | tf_op jit(solution)/shard_map/dot_general | solution.py:138
  (5 shorter events, 0.1 us)
Async XLA Ops:
  7.2 153.8 %copy-start = (f32[1,2048]{1,0:T(1,128)S(1)}, f32[1,2048]{1,0:T(1,128)}, u32[]{:S(2)}) copy-start(f32[1,2048]{1,0:T(1,128)} %param.17) | copy-start | bytes 24580
  7.2 24.3 %copy-start.1 = (f32[1,1,32,2048]{3,2,1,0:T(8,128)S(1)}, f32[1,1,32,2048]{3,2,1,0:T(8,128)}, u32[]{:S(2)}) copy-start(f32[1,1,32,2048]{3,2,1,0:T(8,128)} %param.9) | copy-start | bytes 786436
  7.2 24.3 %copy-start.4 = (f32[1,1,32,2048]{3,2,1,0:T(8,128)S(1)}, f32[1,1,32,2048]{3,2,1,0:T(8,128)}, u32[]{:S(2)}) copy-start(f32[1,1,32,2048]{3,2,1,0:T(8,128)} %param.10) | copy-start | bytes 786436
  7.2 25.2 %copy-start.3 = (s32[1,2,32,2048]{3,2,1,0:T(8,128)S(1)}, s32[1,2,32,2048]{3,2,1,0:T(8,128)}, u32[]{:S(2)}) copy-start(s32[1,2,32,2048]{3,2,1,0:T(8,128)} %param.12) | copy-start | bytes 1572868
  7.2 94.8 %all-gather.3.cloned.1.call-start = ((), (), s32[]{:S(2)}) async-start(), calls=%async_computation.3 | async-start | bytes 2359296 | tf_op jit(solution)/shard_map/all_gather | solution.py:41
  8.2 7.5 %collective-permute-start = (f32[1,2,2048]{2,1,0:T(2,128)S(1)}, f32[1,2,2048]{2,1,0:T(2,128)S(1)}, u32[]{:S(2)}, u32[]{:S(2)}) collective-permute-start(f32[1,2,2048]{2,1,0:T(2,128)S(1)} %get-tuple-element.11), channel_id=1, source_target_pairs={{0,1},{1,2},{2,3},{3,4},{4,5},{5,6},{6,7},{7,8},{8,9},{9,10},{10,1... | collective-permute-start | bytes 49160 | tf_op jit(solution)/shard_map/ppermute | solution.py:18
  10.2 5.6 %collective-permute-start.1 = (f32[1,2,2048]{2,1,0:T(2,128)S(1)}, f32[1,2,2048]{2,1,0:T(2,128)S(1)}, u32[]{:S(2)}, u32[]{:S(2)}) collective-permute-start(f32[1,2,2048]{2,1,0:T(2,128)S(1)} %get-tuple-element.10), channel_id=1, source_target_pairs={{1,0},{2,1},{3,2},{4,3},{5,4},{6,5},{7,6},{8,7},{9,8},{10,9},{11,1... | collective-permute-start | bytes 49160 | tf_op jit(solution)/shard_map/ppermute | solution.py:21
  18.9 12.6 %collective-permute-start.2 = (f32[1,32,2048]{2,1,0:T(8,128)S(1)}, f32[1,32,2048]{2,1,0:T(8,128)S(1)}, u32[]{:S(2)}, u32[]{:S(2)}) collective-permute-start(f32[1,32,2048]{2,1,0:T(8,128)S(1)} %multiply_add_fusion), channel_id=1, source_target_pairs={{0,32},{32,64},{64,96},{96,128},{128,160},{160,192},{192,224},{224... | collective-permute-start | bytes 786440 | tf_op jit(solution)/shard_map/ppermute | solution.py:29
  32.4 81.6 %copy-start.2 = (f32[1,32,2048]{2,1,0:T(8,128)S(1)}, f32[1,32,2048]{2,1,0:T(8,128)}, u32[]{:S(2)}) copy-start(f32[1,32,2048]{2,1,0:T(8,128)} %bitcast_add_fusion) | copy-start | bytes 786436
  32.4 81.6 %copy-start.5 = (f32[1,2,1,32,2048]{4,3,2,1,0:T(8,128)S(1)}, f32[1,2,1,32,2048]{4,3,2,1,0:T(8,128)}, u32[]{:S(2)}) copy-start(f32[1,2,1,32,2048]{4,3,2,1,0:T(8,128)} %param.11) | copy-start | bytes 1572868
  139.6 33.8 %copy-start.6 = (f32[1,1024]{1,0:T(1,128)S(1)}, f32[1,1024]{1,0:T(1,128)}, u32[]{:S(2)}) copy-start(f32[1,1024]{1,0:T(1,128)} %param.16) | copy-start | bytes 12292
  147.7 24.1 %all-to-all-start.1 = ((f32[16,1,4096]{2,1,0:T(1,128)}), f32[16,1,4096]{2,1,0:T(1,128)S(1)}, u32[]{:S(2)}, u32[]{:S(2)}) async-start(f32[16,1,4096]{2,1,0:T(1,128)} %reshape.751), calls=%async_computation.1 | async-start | bytes 524288 | tf_op jit(solution)/shard_map/all_to_all | solution.py:66
Sparse Core Ops, SparseCore 0:
  32.4 47.5 all-gather.2
where the time goes:
time: 320 us; the launch traced here: 319 us
  matrix products  143 us (45%)
  other arithmetic  80.8 us (25%)
  blocking collectives  31 us (10%)
  starting transfers between devices  22.4 us (7%)
  waiting for transfers between devices  19.9 us (6%)
  between operations  16.3 us (5%)
  local copies, waits for them, and re-layouts  5.89 us (2%)
    dot_general x1, matrix products, per_device(): increment = jnp.matmul(spectral, h_lon, precision=high) / (nlat * nlon)  76 us
    add x1, other arithmetic, hartley(): return jnp.cos(angle) + jnp.sin(angle)  69.5 us
    dot_general x1, matrix products, per_device(): spectral = jnp.matmul(resid, h_lon, precision=high)  25.6 us
    dot_general x1, matrix products, per_device(): jnp.einsum('ij,ljk->lik', h_lat, spectral, precision=high) * weight  20.7 us
    dot_general x1, matrix products, per_device(): spectral = jnp.einsum('ij,ljk->lik', h_lat, spectral, precision=high)  20.6 us
    all_to_all x1, blocking collectives, per_device(): lax.all_to_all(spectral, LAT, split_axis=1, concat_axis=2, tiled=True)  16.3 us
    all_to_all x1, starting transfers between devices, moved_by_axis(): lax.all_to_all(tiles, axes[k], split_axis=k, concat_axis=k, tiled=True)  13.3 us
    all_to_all x1, waiting for transfers between devices, moved_by_axis(): lax.all_to_all(tiles, axes[k], split_axis=k, concat_axis=k, tiled=True)  10.7 us
  transfers between devices with their start and end apart: 5, of which 2 were waited for; matrix products, arithmetic and copies ran while one was open for 22% of the time, Pallas kernels for 0%

commit v1 on v0

v1 whole, which is shorter than its diff:
```python
import functools
import math

import jax
import jax.numpy as jnp
import numpy as np
from jax import lax
from jax.experimental import pallas as pl
from jax.experimental.pallas import tpu as pltpu
from jax.sharding import Mesh
from jax.sharding import PartitionSpec as P

AXES = ("win_0", "win_1", "lat_0", "lat_1", "lat_2")
WIN = AXES[:2]
LAT = AXES[2:]
F32 = jnp.float32
BF16 = jnp.bfloat16
AROUND = (4, 5, 3, 6, 2, 7, 1, 0)
TILE_OF = (1, 0, 2, 3)


def rotated(c, s, angle):
    if s is None:
        return c * math.cos(angle), c * math.sin(angle)
    cos, sin = math.cos(angle), math.sin(angle)
    return c * cos - s * sin, c * sin + s * cos


def rfft(xs):
    n = len(xs)
    if n == 2:
        return [(xs[0] + xs[1], None), (xs[0] - xs[1], None)]
    even, odd = rfft(xs[0::2]), rfft(xs[1::2])
    out = [None] * (n // 2 + 1)
    for k in range(n // 4 + 1):
        (ec, es), (oc, os) = even[k], odd[k]
        if k == 0:
            out[0] = (ec + oc, None)
            out[n // 2] = (ec - oc, None)
        elif k == n // 4:
            out[k] = (ec, oc)
        else:
            tc, ts = rotated(oc, os, 2 * math.pi * k / n)
            if es is None:
                out[k] = (ec + tc, ts)
                out[n // 2 - k] = (ec - tc, ts)
            else:
                out[k] = (ec + tc, es + ts)
                out[n // 2 - k] = (ec - tc, ts - es)
    return out


def synth(n, c, s):
    if n == 2:
        return [c[0] + c[1], c[0] - c[1]]
    half, quarter = n // 2, n // 4
    ec, es, oc, os = [], [], [], []
    for k in range(quarter + 1):
        if k == quarter:
            ec.append(c[k])
            es.append(None)
            oc.append(s[k])
            os.append(None)
        elif k == 0:
            ec.append(c[0] + c[half])
            es.append(None)
            oc.append(c[0] - c[half])
            os.append(None)
        else:
            cos, sin = math.cos(2 * math.pi * k / n), math.sin(2 * math.pi * k / n)
            ec.append(c[k] + c[half - k])
            es.append(s[k] - s[half - k])
            dc, ds = c[k] - c[half - k], s[k] + s[half - k]
            oc.append(dc * cos + ds * sin)
            os.append(ds * cos - dc * sin)
    out = [None] * n
    out[0::2] = synth(half, ec, es)
    out[1::2] = synth(half, oc, os)
    return out


def analyse(xs, cos, sin):
    n = len(xs)
    bins = rfft(xs)
    u, v = [], []
    for k in range(n):
        c, s = bins[k] if k <= n // 2 else bins[n - k]
        if k == 0:
            u.append(c)
            v.append(c * 0.0)
        elif s is None:
            u.append(c * cos[k])
            v.append(c * sin[k])
        elif k <= n // 2:
            u.append(c * cos[k] - s * sin[k])
            v.append(c * sin[k] + s * cos[k])
        else:
            u.append(c * cos[k] + s * sin[k])
            v.append(c * sin[k] - s * cos[k])
    return u, v


def synthesise(u, v, cos, sin):
    n = len(u)
    c, s = [u[0]], [None]
    for k in range(1, n):
        c.append(u[k] * cos[k] + v[k] * sin[k])
        s.append(None if k == n // 2 else v[k] * cos[k] - u[k] * sin[k])
    half = n // 2
    fc = [c[0]] + [c[k] + c[n - k] for k in range(1, half)] + [c[half]]
    fs = [None] + [s[k] - s[n - k] for k in range(1, half)] + [None]
    return synth(n, fc, fs)


def twiddle(n1, n2):
    angle = 2 * np.pi * np.arange(n1)[:, None] * np.arange(n2)[None] / (n1 * n2)
    return np.cos(angle), np.sin(angle)


def casmat(n2):
    angle = 2 * np.pi * (np.arange(n2)[:, None] * np.arange(n2)[None] % n2) / n2
    cos, sin = np.cos(angle), np.sin(angle)
    return np.concatenate([cos + sin, cos - sin], 0)


def tables(n1, n2):
    copies = 128 // n2
    cos, sin = (np.tile(t, (1, copies)) for t in twiddle(n1, n2))
    one = casmat(n2)
    eye = np.eye(copies)
    full = np.concatenate([np.kron(eye, one[:n2]), np.kron(eye, one[n2:])], 0)
    return np.concatenate([cos, sin], 0).astype(np.float32), full.astype(np.float32)


def halves(full):
    import ml_dtypes

    hi = full.astype(ml_dtypes.bfloat16)
    lo = (full - hi.astype(np.float32)).astype(ml_dtypes.bfloat16)
    return np.stack([hi, lo])


def dot3(a, hi, lo):
    a_hi = a.astype(BF16)
    a_lo = (a - a_hi.astype(F32)).astype(BF16)
    dot = functools.partial(jnp.dot, preferred_element_type=F32)
    return dot(a_hi, hi) + (dot(a_lo, hi) + dot(a_hi, lo))


def gathered(spec, n1, n2):
    n = n1 * n2
    rows = lax.broadcasted_iota(jnp.int32, (n1, n), 0)
    lanes = lax.broadcasted_iota(jnp.int32, (n1, n), 1)
    own = jnp.where((lanes & (n1 - 1)) == rows, jnp.broadcast_to(spec, (n1, n)), 0.0)
    first = own.astype(BF16)
    rest = own - first.astype(F32)
    second = rest.astype(BF16)
    third = (rest - second.astype(F32)).astype(BF16)
    place = lax.broadcasted_iota(jnp.int32, (n, 128), 0) >> (n1.bit_length() - 1)
    lane = lax.broadcasted_iota(jnp.int32, (n, 128), 1) & (n2 - 1)
    pick = jnp.where(place == lane, 1.0, 0.0).astype(BF16)
    dot = functools.partial(jnp.dot, preferred_element_type=F32)
    return dot(first, pick) + dot(second, pick) + dot(third, pick)


def slot_of(tile, group):
    return (group // 2) * 8 + (group % 2) * 4 + TILE_OF.index(tile)


def kernel(
    state, mult, obs, mask, speed, drift, kappa, lat_spec, lon_spec, tw, wf, wb,
    new_state, new_mult,
    xb, mb, ob, kb, ls, lo, twb, wfb, wbb,
    halo, x1b, x2b, pb, lb, lamb, a_out, a_in, p_out, p_in,
    rb, tb, zb, yb, ob2, vb, uv, lsf, lnf, outb,
    in_sem, out_sem, h_send, h_recv, a_send, a_recv, p_send, p_recv, e_send, e_recv, z_send, z_recv, y_send, y_recv,
):
    xh, y, z, xl, core = (lax.axis_index(a) for a in AXES)
    w = xh * 8 + y
    l = z * 4 + xl * 2 + core
    group = xl * 2 + core

    def at_win(v):
        return (lax.div(v, 8), lax.rem(v, 8), z, xl, core)

    def at_lat(m):
        return (xh, y, lax.div(m, 4), lax.rem(lax.div(m, 2), 2), lax.rem(m, 2))

    loads = [
        pltpu.make_async_copy(src, dst, in_sem.at[i])
        for i, (src, dst) in enumerate(
            [(state, xb), (mult, mb), (obs, ob), (mask, kb), (lat_spec, ls), (lon_spec, lo), (tw, twb), (wf, wfb), (wb, wbb)]
        )
    ]
    for load in loads:
        load.start()

    barrier = pltpu.get_barrier_semaphore()
    for k in range(1, 16):
        pl.semaphore_signal(barrier, inc=1, device_id=at_win(lax.rem(w + k, 16)), device_id_type=pl.DeviceIdType.MESH)
    for k in range(1, 32):
        pl.semaphore_signal(barrier, inc=1, device_id=at_lat(lax.rem(l + k, 32)), device_id_type=pl.DeviceIdType.MESH)

    sends = []

    def send(src, dst, send_sem, recv_sem, device, when=None):
        copy = pltpu.make_async_remote_copy(
            src_ref=src, dst_ref=dst, send_sem=send_sem, recv_sem=recv_sem,
            device_id=device, device_id_type=pl.DeviceIdType.MESH,
        )
        guarded(when, copy.start)
        sends.append((when, copy))

    def guarded(when, act):
        if when is None:
            act()
        else:
            pl.when(when)(act)

    def arrived(dst, recv_sem, send_sem, device, when=None):
        copy = pltpu.make_async_remote_copy(
            src_ref=dst, dst_ref=dst, send_sem=send_sem, recv_sem=recv_sem,
            device_id=device, device_id_type=pl.DeviceIdType.MESH,
        )
        guarded(when, copy.wait_recv)

    sp, dr, ka = speed[0], drift[0], kappa[0]
    row = lax.broadcasted_iota(jnp.int32, (8, 2048), 0)
    later = jnp.where(w > 0, F32(0.5), F32(0.0))
    inv = F32(1.0)
    for k in range(2, 16):
        inv = jnp.where(w == k, F32(1.0 / k), inv)

    def step(mid, north, south):
        east = pltpu.roll(mid, 2047, 1)
        west = pltpu.roll(mid, 1, 1)
        return (
            mid
            - (sp * mid * (east - west)) * 0.5
            - (dr * (north - south)) * 0.5
            + ka * (east + west + north + south - 4.0 * mid)
        )

    def up(t):
        return pltpu.roll(t, 7, 0)

    def down(t):
        return pltpu.roll(t, 1, 0)

    def advanced(before, mid, after):
        u, d = up(mid), down(mid)
        north = u if after is None else jnp.where(row == 7, up(after), u)
        south = d if before is None else jnp.where(row == 0, down(before), d)
        return step(mid, north, south)

    def tile(ref, t):
        return ref[8 * t : 8 * t + 8, :]

    def finish_tile(t, second):
        a = tile(mb, t) + later * tile(xb, t) - 0.5 * second
        for g in range(4):
            a_out[slot_of(t, g)] = a[:, 512 * g : 512 * g + 512]
            x2b[g, 8 * t : 8 * t + 8, :] = second[:, 512 * g : 512 * g + 512]

    def send_a(odd):
        for off in (2, 1, 3, 0):
            yy = 2 * lax.rem(lax.div(y, 2) + off, 4) + odd
            for far in (1, 0):
                owner = lax.rem(xh + far, 2) * 8 + yy
                when = (lax.rem(y, 2) != odd) if (off == 0 and far == 0) else None
                send(a_out.at[owner], a_in.at[w], a_send.at[owner], a_recv.at[w], at_win(owner), when)

    loads[0].wait()
    first = [tile(xb, t) for t in range(4)]
    for t in range(4):
        x1b[8 * t : 8 * t + 8, :] = advanced(
            first[t - 1] if t > 0 else None, first[t], first[t + 1] if t < 3 else None
        )
    loads[1].wait()
    pl.semaphore_wait(barrier, 46)
    north_of, south_of = lax.rem(l + 1, 32), lax.rem(l + 31, 32)
    send(xb.at[24:32, :], halo.at[0], h_send.at[0], h_recv.at[0], at_lat(north_of), l < 31)
    send(xb.at[0:8, :], halo.at[1], h_send.at[1], h_recv.at[1], at_lat(south_of), l > 0)
    for t in (1, 2):
        finish_tile(t, advanced(tile(x1b, t - 1), tile(x1b, t), tile(x1b, t + 1)))
    send_a(0)

    @pl.when(l == 0)
    def _():
        halo[0] = jnp.zeros((8, 2048), F32)

    @pl.when(l == 31)
    def _():
        halo[1] = jnp.zeros((8, 2048), F32)

    arrived(halo.at[0], h_recv.at[0], h_send.at[0], at_lat(south_of), l > 0)
    arrived(halo.at[1], h_recv.at[1], h_send.at[1], at_lat(north_of), l < 31)
    low, high = halo[0], halo[1]
    beyond_low = jnp.where(l > 0, advanced(None, low, tile(xb, 0)), 0.0)
    edge = advanced(low, tile(xb, 0), tile(xb, 1))
    x1b[0:8, :] = edge
    finish_tile(0, advanced(beyond_low, edge, tile(x1b, 1)))
    beyond_high = jnp.where(l < 31, advanced(tile(xb, 3), high, None), 0.0)
    edge = advanced(tile(xb, 2), tile(xb, 3), high)
    x1b[24:32, :] = edge
    finish_tile(3, advanced(tile(x1b, 2), edge, beyond_high))
    send_a(1)
    for g in range(4):
        send(x2b.at[g], pb.at[g], e_send.at[g], e_recv.at[g], at_win(lax.rem(w + 1, 16)), w < 15)
    a_in[w] = a_out[w]

    loads[2].wait()
    loads[3].wait()
    for t in range(4):
        rows = slice(8 * t, 8 * t + 8)
        second = jnp.concatenate([x2b[g, rows, :] for g in range(4)], axis=1)
        lb[rows, :] = (
            kb[0, rows, :].astype(F32) * (ob[0, rows, :] - x1b[rows, :])
            + kb[1, rows, :].astype(F32) * (ob[1, rows, :] - second)
            + (mb[rows, :] + later * xb[rows, :])
        )

    for k in range(1, 16):
        v = lax.rem(w + k, 16)
        arrived(a_in.at[v], a_recv.at[v], a_send.at[v], at_win(v))
    total = jnp.zeros((8, 512), F32)
    for v in range(16):
        p_out[v] = total
        if v < 15:
            total = total + a_in[v]
    for off in AROUND:
        for far in (1, 0):
            if off or far:
                v = lax.rem(xh + far, 2) * 8 + lax.rem(y + off, 8)
                send(p_out.at[v], p_in.at[w], p_send.at[v], p_recv.at[w], at_win(v))
    p_in[w] = p_out[w]

    for load in loads[4:]:
        load.wait()
    for ref, out, n1, n2, scale in ((ls, lsf, 32, 32, 2.0**-22), (lo, lnf, 16, 128, 1.0)):
        spread = gathered(ref[...], n1, n2) * scale
        depth = 512 // n1
        for k in range(n1):
            out[depth * k : depth * (k + 1), :] = jnp.broadcast_to(spread[k : k + 1, :], (depth, 128))

    @pl.when(w == 0)
    def _():
        pb[...] = jnp.zeros((4, 32, 512), F32)

    for g in range(4):
        for t in range(4):
            owner = slot_of(t, g)
            arrived(p_in.at[owner], p_recv.at[owner], p_send.at[owner], at_win(owner * 1 + 0 * w), w != owner)
        arrived(pb.at[g], e_recv.at[g], e_send.at[g], at_win(lax.rem(w + 15, 16)), w > 0)
        columns = slice(512 * g, 512 * g + 512)
        for t in range(4):
            rows = slice(8 * t, 8 * t + 8)
            prior = 0.5 * pb[g, rows, :]
            lamb[rows, columns] = mb[rows, columns] + later * xb[rows, columns] - prior
            r = lb[rows, columns] - prior - (p_in[slot_of(t, g)] + prior) * inv
            for c in range(4):
                rb[32 * c + 8 * t : 32 * c + 8 * t + 8, :] = r[:, 128 * c : 128 * c + 128]
        tb[g] = rb[...].T
        for off in AROUND:
            to = lax.rem(z + off, 8)
            target = to * 4 + g
            when = None if off else (group != g)
            send(
                tb.at[g, pl.ds(pl.multiple_of(to * 16, 16), 16), :], zb.at[l],
                z_send.at[target], z_recv.at[l], at_lat(target), when,
            )
    zb[l] = tb[group, pl.ds(pl.multiple_of(z * 16, 16), 16), :]
    save = pltpu.make_async_copy(lamb, new_mult, out_sem.at[0])
    save.start()

    for k in range(1, 32):
        m = lax.rem(l + k, 32)
        arrived(zb.at[m], z_recv.at[m], z_send.at[m], at_lat(m))

    def operator(n1, depth, source, sink, cos_at, sin_at, table, scale):
        cos = [twb[cos_at + k : cos_at + k + 1, :] for k in range(n1)]
        sin = [twb[sin_at + k : sin_at + k + 1, :] for k in range(n1)]
        for h in range(depth // 8):
            u, v = analyse([source(j, h) for j in range(n1)], cos, sin)
            for k in range(n1):
                at = depth * k + 8 * h
                uv[at : at + 8, 0:128] = u[k]
                uv[at : at + 8, 128:256] = v[k]
        for q in range(4):
            rows = slice(128 * q, 128 * q + 128)
            spectral = dot3(uv[rows, :], wfb[table, 0], wfb[table, 1]) * scale[rows, :]
            uv[rows, :] = dot3(spectral, wbb[table, 0], wbb[table, 1])
        for h in range(depth // 8):
            at = [depth * k + 8 * h for k in range(n1)]
            out = synthesise([uv[a : a + 8, 0:128] for a in at], [uv[a : a + 8, 128:256] for a in at], cos, sin)
            for j in range(n1):
                sink(j, h, out[j])

    def lat_sink(j, h, value):
        ob2[j, 8 * h : 8 * h + 8, :] = value

    operator(32, 16, lambda j, h: zb[j, 8 * h : 8 * h + 8, :], lat_sink, 0, 32, 0, lsf)
    here = pl.ds(pl.multiple_of(z * 16, 16), 16)
    for off in AROUND:
        for near in (2, 3, 1, 0):
            if off or near:
                m = lax.rem(z + off, 8) * 4 + lax.rem(group + near, 4)
                send(ob2.at[m], yb.at[group, here, :], y_send.at[m], y_recv.at[l], at_lat(m))
    yb[group, here, :] = ob2[l]

    for k in range(1, 32):
        m = lax.rem(l + k, 32)
        there = pl.ds(pl.multiple_of(lax.div(m, 4) * 16, 16), 16)
        arrived(yb.at[lax.rem(m, 4), there, :], y_recv.at[m], y_send.at[m], at_lat(m))
    for g in range(4):
        turned = yb[g].T
        for c in range(4):
            vb[4 * g + c] = turned[32 * c : 32 * c + 32, :]

    def lon_sink(j, h, value):
        rows, columns = slice(8 * h, 8 * h + 8), slice(128 * j, 128 * j + 128)
        outb[rows, columns] = xb[rows, columns] + value

    operator(16, 32, lambda j, h: vb[j, 8 * h : 8 * h + 8, :], lon_sink, 64, 80, 1, lnf)
    result = pltpu.make_async_copy(outb, new_state, out_sem.at[1])
    result.start()
    for when, copy in sends:
        guarded(when, copy.wait_send)
    save.wait()
    result.wait()


def per_device(state, multipliers, observations, obs_mask, speed, drift, kappa, lat_spectrum, lon_spectrum):
    band, nlon = state.shape[2:]
    tw_lat, w_lat = tables(32, 32)
    tw_lon, w_lon = tables(16, 128)
    tw = jnp.asarray(np.concatenate([tw_lat, tw_lon], 0))
    wf = jnp.asarray(np.stack([halves(w_lat), halves(w_lon)]))
    wb = jnp.asarray(np.stack([halves(np.ascontiguousarray(w_lat.T)), halves(np.ascontiguousarray(w_lon.T))]))
    hbm = pl.BlockSpec(memory_space=pltpu.HBM)
    smem = pl.BlockSpec(memory_space=pltpu.SMEM)
    vmem = pltpu.VMEM
    dma = pltpu.SemaphoreType.DMA
    new_state, new_mult = pl.pallas_call(
        kernel,
        out_shape=[jax.ShapeDtypeStruct((band, nlon), F32)] * 2,
        in_specs=[hbm] * 4 + [smem] * 3 + [hbm] * 5,
        out_specs=[hbm] * 2,
        scratch_shapes=[
            vmem((32, 2048), F32), vmem((32, 2048), F32), vmem((2, 32, 2048), F32), vmem((2, 32, 2048), jnp.int32),
            vmem((1, 1024), F32), vmem((1, 2048), F32), vmem((96, 128), F32),
            vmem((2, 2, 256, 128), BF16), vmem((2, 2, 128, 256), BF16),
            vmem((2, 8, 2048), F32), vmem((32, 2048), F32), vmem((4, 32, 512), F32), vmem((4, 32, 512), F32),
            vmem((32, 2048), F32), vmem((32, 2048), F32),
            vmem((16, 8, 512), F32), vmem((16, 8, 512), F32), vmem((16, 8, 512), F32), vmem((16, 8, 512), F32),
            vmem((128, 128), F32), vmem((4, 128, 128), F32), vmem((32, 16, 128), F32),
            vmem((4, 128, 128), F32), vmem((32, 16, 128), F32), vmem((16, 32, 128), F32), vmem((512, 256), F32),
            vmem((512, 128), F32), vmem((512, 128), F32), vmem((32, 2048), F32),
            dma((9,)), dma((2,)), dma((2,)), dma((2,)), dma((16,)), dma((16,)), dma((16,)), dma((16,)),
            dma((4,)), dma((4,)), dma((32,)), dma((32,)), dma((32,)), dma((32,)),
        ],
        compiler_params=pltpu.CompilerParams(
            collective_id=0, has_side_effects=True, vmem_limit_bytes=40 * 1024 * 1024
        ),
        name="saddle_step",
    )(
        state[0, 0], multipliers[0, 0], observations[0, :, 0], obs_mask[0], speed, drift, kappa,
        lat_spectrum, lon_spectrum, tw, wf, wb,
    )
    return new_state[None, None], new_mult[None, None]


def solution(mesh):
    finer = Mesh(mesh.devices.reshape(2, 8, 8, 2, 2), AXES)
    placed = (
        P(WIN, None, LAT, None),
        P(WIN, None, LAT, None),
        P(WIN, None, None, LAT, None),
        P(WIN, None, LAT, None),
        P(),
        P(),
        P(),
        P(),
        P(),
    )
    return jax.shard_map(
        per_device,
        mesh=finer,
        in_specs=placed,
        out_specs=(P(WIN, None, LAT, None), P(WIN, None, LAT, None)),
        check_vma=False,
    )
```

time: 320 us -> 67.6 us (0.21)
  the two profiles are of different devices: /device:TPU:6 before, /device:TPU:9 now
where the time goes in v1:
time: 67.6 us; the launch traced here: 67.1 us
  Pallas kernels  55.7 us (82%)
  local copies, waits for them, and re-layouts  8.76 us (13%)
  between operations  2.62 us (4%)
    pallas_call x1, Pallas kernels, per_device(): pl.pallas_call(kernel, out_shape=[jax.ShapeDtypeStruct((band, nlon), F32)...  55.7 us
    unnamed x20, local copies, waits for them, and re-layouts  8.76 us

profile of v1, /device:TPU:9, one launch (start us, length us, event | category | flops | bytes accessed | tf_op | source)
XLA Modules:
  0.0 67.1 jit_solution(1380737692668027245)
XLA Ops:
  0.6 0.0 copy-start.7
  2.6 0.0 copy-start.8
  2.6 0.0 copy-done.7
  2.6 0.7 copy-done.8
  3.3 0.0 copy-start
  3.3 1.0 %copy-done = f32[1,2,1,32,2048]{4,3,2,1,0:T(8,128)S(1)} copy-done((f32[1,2,1,32,2048]{4,3,2,1,0:T(8,128)S(1)}, f32[1,2,1,32,2048]{4,3,2,1,0:T(8,128)}, u32[]{:S(2)}) %copy-start) | copy-done | bytes 524312
  4.3 0.0 copy-start.1
  4.3 1.0 %copy-done.1 = s32[1,2,32,2048]{3,2,1,0:T(8,128)S(1)} copy-done((s32[1,2,32,2048]{3,2,1,0:T(8,128)S(1)}, s32[1,2,32,2048]{3,2,1,0:T(8,128)}, u32[]{:S(2)}) %copy-start.1) | copy-done | bytes 524312
  5.4 0.0 copy-start.2
  5.4 0.9 %copy-done.2 = f32[1,1,32,2048]{3,2,1,0:T(8,128)S(1)} copy-done((f32[1,1,32,2048]{3,2,1,0:T(8,128)S(1)}, f32[1,1,32,2048]{3,2,1,0:T(8,128)}, u32[]{:S(2)}) %copy-start.2) | copy-done | bytes 262168
  6.3 0.0 copy-start.3
  6.3 0.9 %copy-done.3 = f32[1,1,32,2048]{3,2,1,0:T(8,128)S(1)} copy-done((f32[1,1,32,2048]{3,2,1,0:T(8,128)S(1)}, f32[1,1,32,2048]{3,2,1,0:T(8,128)}, u32[]{:S(2)}) %copy-start.3) | copy-done | bytes 262168
  7.3 0.0 copy-start.4
  7.3 0.9 %copy-done.4 = bf16[2,2,128,256]{3,2,1,0:T(8,128)(2,1)S(1)} copy-done((bf16[2,2,128,256]{3,2,1,0:T(8,128)(2,1)S(1)}, bf16[2,2,128,256]{3,2,1,0:T(8,128)(2,1)}, u32[]{:S(2)}) %copy-start.4) | copy-done | bytes 262168
  8.2 0.0 copy-start.5
  8.2 0.9 %copy-done.5 = bf16[2,2,256,128]{3,2,1,0:T(8,128)(2,1)S(1)} copy-done((bf16[2,2,256,128]{3,2,1,0:T(8,128)(2,1)S(1)}, bf16[2,2,256,128]{3,2,1,0:T(8,128)(2,1)}, u32[]{:S(2)}) %copy-start.5) | copy-done | bytes 262168
  9.2 0.0 copy-start.6
  9.2 0.8 %copy-done.6 = f32[96,128]{1,0:T(8,128)S(1)} copy-done((f32[96,128]{1,0:T(8,128)S(1)}, f32[96,128]{1,0:T(8,128)}, u32[]{:S(2)}) %copy-start.6) | copy-done | bytes 49176
  10.0 55.7 %saddle_step.1 = (f32[32,2048]{1,0:T(8,128)S(1)}, f32[32,2048]{1,0:T(8,128)S(1)}) custom-call(f32[32,2048]{1,0:T(8,128)S(1)} %bitcast.8, f32[32,2048]{1,0:T(8,128)S(1)} %bitcast.9, f32[2,32,2048]{2,1,0:T(8,128)S(1)} %bitcast.6, s32[2,32,2048]{2,1,0:T(8,128)S(1)} %bitcast.7, f32[1]{0:T(128)S(6)} %copy.16.speed, f32[1]{0:T(128)S(6)} %copy.17.drift, ...), custom_call_target="tpu_custom_call" | custom-call | tf_op jit(solution)/shard_map/saddle_step/pallas_call | solution.py:444
  65.7 0.7 %copy.19 = f32[1,1,32,2048]{3,2,1,0:T(8,128)} copy(f32[1,1,32,2048]{3,2,1,0:T(8,128)S(1)} %bitcast.11) | data formatting | bytes 524288
  66.4 0.7 %copy.20 = f32[1,1,32,2048]{3,2,1,0:T(8,128)} copy(f32[1,1,32,2048]{3,2,1,0:T(8,128)S(1)} %bitcast.10) | data formatting | bytes 524288
Async XLA Ops:
  0.6 2.0 %copy-start.7 = (f32[1,2048]{1,0:T(1,128)S(1)}, f32[1,2048]{1,0:T(1,128)}, u32[]{:S(2)}) copy-start(f32[1,2048]{1,0:T(1,128)} %lon_spec.1) | copy-start | bytes 24580
  2.6 0.7 %copy-start.8 = (f32[1,1024]{1,0:T(1,128)S(1)}, f32[1,1024]{1,0:T(1,128)}, u32[]{:S(2)}) copy-start(f32[1,1024]{1,0:T(1,128)} %lat_spec.1) | copy-start | bytes 12292
  3.3 1.0 %copy-start = (f32[1,2,1,32,2048]{4,3,2,1,0:T(8,128)S(1)}, f32[1,2,1,32,2048]{4,3,2,1,0:T(8,128)}, u32[]{:S(2)}) copy-start(f32[1,2,1,32,2048]{4,3,2,1,0:T(8,128)} %param.14) | copy-start | bytes 1572868
  4.3 1.0 %copy-start.1 = (s32[1,2,32,2048]{3,2,1,0:T(8,128)S(1)}, s32[1,2,32,2048]{3,2,1,0:T(8,128)}, u32[]{:S(2)}) copy-start(s32[1,2,32,2048]{3,2,1,0:T(8,128)} %param.15) | copy-start | bytes 1572868
  5.4 0.9 %copy-start.2 = (f32[1,1,32,2048]{3,2,1,0:T(8,128)S(1)}, f32[1,1,32,2048]{3,2,1,0:T(8,128)}, u32[]{:S(2)}) copy-start(f32[1,1,32,2048]{3,2,1,0:T(8,128)} %param.12) | copy-start | bytes 786436
  6.3 0.9 %copy-start.3 = (f32[1,1,32,2048]{3,2,1,0:T(8,128)S(1)}, f32[1,1,32,2048]{3,2,1,0:T(8,128)}, u32[]{:S(2)}) copy-start(f32[1,1,32,2048]{3,2,1,0:T(8,128)} %param.13) | copy-start | bytes 786436
  7.3 0.9 %copy-start.4 = (bf16[2,2,128,256]{3,2,1,0:T(8,128)(2,1)S(1)}, bf16[2,2,128,256]{3,2,1,0:T(8,128)(2,1)}, u32[]{:S(2)}) copy-start(bf16[2,2,128,256]{3,2,1,0:T(8,128)(2,1)} %constant.8.clone.wb) | copy-start | bytes 786436
  8.2 0.9 %copy-start.5 = (bf16[2,2,256,128]{3,2,1,0:T(8,128)(2,1)S(1)}, bf16[2,2,256,128]{3,2,1,0:T(8,128)(2,1)}, u32[]{:S(2)}) copy-start(bf16[2,2,256,128]{3,2,1,0:T(8,128)(2,1)} %constant.7.clone.wf) | copy-start | bytes 786436
  9.2 0.8 %copy-start.6 = (f32[96,128]{1,0:T(8,128)S(1)}, f32[96,128]{1,0:T(8,128)}, u32[]{:S(2)}) copy-start(f32[96,128]{1,0:T(8,128)} %constant.6.clone.tw) | copy-start | bytes 147460

commit v2 on v1

v2 whole, which is shorter than its diff:
```python
import functools
import math

import jax
import jax.numpy as jnp
import numpy as np
from jax import lax
from jax.experimental import pallas as pl
from jax.experimental.pallas import tpu as pltpu
from jax.sharding import Mesh
from jax.sharding import PartitionSpec as P

AXES = ("win_0", "win_1", "lat_0", "lat_1", "lat_2")
WIN = AXES[:2]
LAT = AXES[2:]
F32 = jnp.float32
BF16 = jnp.bfloat16
AROUND = (4, 5, 3, 6, 2, 7, 1, 0)
TILE_OF = (1, 0, 2, 3)


def rotated(c, s, angle):
    if s is None:
        return c * math.cos(angle), c * math.sin(angle)
    cos, sin = math.cos(angle), math.sin(angle)
    return c * cos - s * sin, c * sin + s * cos


def rfft(xs):
    n = len(xs)
    if n == 2:
        return [(xs[0] + xs[1], None), (xs[0] - xs[1], None)]
    even, odd = rfft(xs[0::2]), rfft(xs[1::2])
    out = [None] * (n // 2 + 1)
    for k in range(n // 4 + 1):
        (ec, es), (oc, os) = even[k], odd[k]
        if k == 0:
            out[0] = (ec + oc, None)
            out[n // 2] = (ec - oc, None)
        elif k == n // 4:
            out[k] = (ec, oc)
        else:
            tc, ts = rotated(oc, os, 2 * math.pi * k / n)
            if es is None:
                out[k] = (ec + tc, ts)
                out[n // 2 - k] = (ec - tc, ts)
            else:
                out[k] = (ec + tc, es + ts)
                out[n // 2 - k] = (ec - tc, ts - es)
    return out


def synth(n, c, s):
    if n == 2:
        return [c[0] + c[1], c[0] - c[1]]
    half, quarter = n // 2, n // 4
    ec, es, oc, os = [], [], [], []
    for k in range(quarter + 1):
        if k == quarter:
            ec.append(c[k])
            es.append(None)
            oc.append(s[k])
            os.append(None)
        elif k == 0:
            ec.append(c[0] + c[half])
            es.append(None)
            oc.append(c[0] - c[half])
            os.append(None)
        else:
            cos, sin = math.cos(2 * math.pi * k / n), math.sin(2 * math.pi * k / n)
            ec.append(c[k] + c[half - k])
            es.append(s[k] - s[half - k])
            dc, ds = c[k] - c[half - k], s[k] + s[half - k]
            oc.append(dc * cos + ds * sin)
            os.append(ds * cos - dc * sin)
    out = [None] * n
    out[0::2] = synth(half, ec, es)
    out[1::2] = synth(half, oc, os)
    return out


def analyse(xs, cos, sin):
    n = len(xs)
    bins = rfft(xs)
    u, v = [], []
    for k in range(n):
        c, s = bins[k] if k <= n // 2 else bins[n - k]
        if k == 0:
            u.append(c)
            v.append(c * 0.0)
        elif s is None:
            u.append(c * cos[k])
            v.append(c * sin[k])
        elif k <= n // 2:
            u.append(c * cos[k] - s * sin[k])
            v.append(c * sin[k] + s * cos[k])
        else:
            u.append(c * cos[k] + s * sin[k])
            v.append(c * sin[k] - s * cos[k])
    return u, v


def synthesise(u, v, cos, sin):
    n = len(u)
    c, s = [u[0]], [None]
    for k in range(1, n):
        c.append(u[k] * cos[k] + v[k] * sin[k])
        s.append(None if k == n // 2 else v[k] * cos[k] - u[k] * sin[k])
    half = n // 2
    fc = [c[0]] + [c[k] + c[n - k] for k in range(1, half)] + [c[half]]
    fs = [None] + [s[k] - s[n - k] for k in range(1, half)] + [None]
    return synth(n, fc, fs)


def twiddle(n1, n2):
    angle = 2 * np.pi * np.arange(n1)[:, None] * np.arange(n2)[None] / (n1 * n2)
    return np.cos(angle), np.sin(angle)


def casmat(n2):
    angle = 2 * np.pi * (np.arange(n2)[:, None] * np.arange(n2)[None] % n2) / n2
    cos, sin = np.cos(angle), np.sin(angle)
    return np.concatenate([cos + sin, cos - sin], 0)


def tables(n1, n2):
    copies = 128 // n2
    cos, sin = (np.tile(t, (1, copies)) for t in twiddle(n1, n2))
    one = casmat(n2)
    eye = np.eye(copies)
    full = np.concatenate([np.kron(eye, one[:n2]), np.kron(eye, one[n2:])], 0)
    return np.concatenate([cos, sin], 0).astype(np.float32), full.astype(np.float32)


def halves(full):
    import ml_dtypes

    hi = full.astype(ml_dtypes.bfloat16)
    lo = (full - hi.astype(np.float32)).astype(ml_dtypes.bfloat16)
    return np.stack([hi, lo])


def dot3(a, hi, lo):
    a_hi = a.astype(BF16)
    a_lo = (a - a_hi.astype(F32)).astype(BF16)
    dot = functools.partial(jnp.dot, preferred_element_type=F32)
    return dot(a_hi, hi) + (dot(a_lo, hi) + dot(a_hi, lo))


def gathered(spec, n1, n2):
    n = n1 * n2
    rows = lax.broadcasted_iota(jnp.int32, (n1, n), 0)
    lanes = lax.broadcasted_iota(jnp.int32, (n1, n), 1)
    own = jnp.where((lanes & (n1 - 1)) == rows, jnp.broadcast_to(spec, (n1, n)), 0.0)
    first = own.astype(BF16)
    rest = own - first.astype(F32)
    second = rest.astype(BF16)
    third = (rest - second.astype(F32)).astype(BF16)
    place = lax.broadcasted_iota(jnp.int32, (n, 128), 0) >> (n1.bit_length() - 1)
    lane = lax.broadcasted_iota(jnp.int32, (n, 128), 1) & (n2 - 1)
    pick = jnp.where(place == lane, 1.0, 0.0).astype(BF16)
    dot = functools.partial(jnp.dot, preferred_element_type=F32)
    return dot(first, pick) + dot(second, pick) + dot(third, pick)


def slot_of(tile, group):
    return (group // 2) * 8 + (group % 2) * 4 + TILE_OF.index(tile)


def operator(source, sink, n1, depth, cos, sin, scale, uv, wf, wb):
    for h in range(depth // 8):
        u, v = analyse([source(j, h) for j in range(n1)], cos, sin)
        for k in range(n1):
            at = depth * k + 8 * h
            uv[at : at + 8, 0:128] = u[k]
            uv[at : at + 8, 128:256] = v[k]
    for q in range(4):
        rows = slice(128 * q, 128 * q + 128)
        factor = jnp.concatenate(
            [jnp.broadcast_to(scale[k : k + 1, :], (depth, 128)) for k in range(128 * q // depth, 128 * (q + 1) // depth)], axis=0
        )
        spectral = dot3(uv[rows, :], wf[0], wf[1]) * factor
        uv[rows, :] = dot3(spectral, wb[0], wb[1])
    for h in range(depth // 8):
        at = [depth * k + 8 * h for k in range(n1)]
        out = synthesise([uv[a : a + 8, 0:128] for a in at], [uv[a : a + 8, 128:256] for a in at], cos, sin)
        for j in range(n1):
            sink(j, h, out[j])


def rows_of(ref, first, count):
    return [ref[first + k : first + k + 1, :] for k in range(count)]


def exchange_kernel(
    state, mult, obs, mask, speed, drift, kappa, lat_spec, lon_spec, tw, wf, wb,
    turned, new_mult, lon_scale,
    xb, mb, ob, kb, ls, lo, twb, wfb, wbb,
    halo, x1b, x2b, pb, lb, lamb, a_out, a_in, p_out, p_in, ea_out, ea_in, ep_out, ep_in, rel,
    rb, tb, zb, ob2, uv, lsf, lnf,
    in_sem, out_sem, h_send, h_recv, a_send, a_recv, p_send, p_recv, ea_send, ea_recv, ep_send, ep_recv,
    e_send, e_recv, rel_send, rel_recv, z_send, z_recv, y_send, y_recv,
):
    xh, y, z, xl, core = (lax.axis_index(a) for a in AXES)
    w = xh * 8 + y
    l = z * 4 + xl * 2 + core
    group = xl * 2 + core

    def at_win(v):
        return (lax.div(v, 8), lax.rem(v, 8), z, xl, core)

    def at_lat(m):
        return (xh, y, lax.div(m, 4), lax.rem(lax.div(m, 2), 2), lax.rem(m, 2))

    loads = [
        pltpu.make_async_copy(src, dst, in_sem.at[i])
        for i, (src, dst) in enumerate(
            [(state, xb), (mult, mb), (obs, ob), (mask, kb), (lat_spec, ls), (lon_spec, lo), (tw, twb), (wf, wfb), (wb, wbb)]
        )
    ]
    for load in loads:
        load.start()

    windows = [lax.rem(xh + far, 2) * 8 + lax.rem(y + off, 8) for off in AROUND for far in (1, 0) if off or far]
    bands = [lax.rem(z + off, 8) * 4 + lax.rem(group + near, 4) for off in AROUND for near in (2, 3, 1, 0) if off or near]
    barrier = pltpu.get_barrier_semaphore()
    for v in windows:
        pl.semaphore_signal(barrier, inc=1, device_id=at_win(v), device_id_type=pl.DeviceIdType.MESH)
    for m in bands:
        pl.semaphore_signal(barrier, inc=1, device_id=at_lat(m), device_id_type=pl.DeviceIdType.MESH)

    def guarded(when, act):
        if when is None:
            act()
        else:
            pl.when(when)(act)

    def send(src, dst, send_sem, recv_sem, device, when=None):
        copy = pltpu.make_async_remote_copy(
            src_ref=src, dst_ref=dst, send_sem=send_sem, recv_sem=recv_sem,
            device_id=device, device_id_type=pl.DeviceIdType.MESH,
        )
        guarded(when, copy.start)

    def wait(like, sem, when=None):
        guarded(when, pltpu.make_async_copy(like, like, sem).wait)

    def wait_either(when, first, second, sem):
        wait(first, sem, when)
        wait(second, sem, jnp.logical_not(when))

    row = lax.broadcasted_iota(jnp.int32, (8, 2048), 0)
    row8 = lax.broadcasted_iota(jnp.int32, (8, 1024), 0)
    row1 = lax.broadcasted_iota(jnp.int32, (8, 128), 0)
    later = jnp.where(w > 0, F32(0.5), F32(0.0))
    inv = F32(1.0)
    for k in range(2, 16):
        inv = jnp.where(w == k, F32(1.0 / k), inv)
    sp, dr, ka = speed[0], drift[0], kappa[0]

    def step(mid, north, south):
        east = pltpu.roll(mid, 2047, 1)
        west = pltpu.roll(mid, 1, 1)
        return (
            mid
            - (sp * mid * (east - west)) * 0.5
            - (dr * (north - south)) * 0.5
            + ka * (east + west + north + south - 4.0 * mid)
        )

    def advanced(before, mid, after):
        north, south = pltpu.roll(mid, 7, 0), pltpu.roll(mid, 1, 0)
        if after is not None:
            north = jnp.where(row == 7, pltpu.roll(after, 7, 0), north)
        if before is not None:
            south = jnp.where(row == 0, pltpu.roll(before, 1, 0), south)
        return step(mid, north, south)

    def tile(ref, t):
        return ref[8 * t : 8 * t + 8, :]

    def keep(t, second):
        for g in range(4):
            for q in range(4):
                at = 512 * g + 128 * q
                x2b[q, 8 * t : 8 * t + 8, 128 * g : 128 * g + 128] = second[:, at : at + 128]

    def term(t, second):
        return tile(mb, t) + later * tile(xb, t) - 0.5 * second

    def send_prior(q, when):
        send(x2b.at[q], pb.at[q], e_send, e_recv.at[q], at_win(lax.rem(w + 1, 16)), when)

    def relay_prior():
        wait(rel, rel_recv)
        for q in (2, 3):
            send(rel.at[q - 2], pb.at[q], rel_send, e_recv.at[q], at_win(jnp.int32(8)))

    loads[0].wait()
    first = [tile(xb, t) for t in range(4)]
    for t in range(4):
        x1b[8 * t : 8 * t + 8, :] = advanced(
            first[t - 1] if t > 0 else None, first[t], first[t + 1] if t < 3 else None
        )
    loads[1].wait()
    for t in range(4):
        second = advanced(
            tile(x1b, t - 1) if t > 0 else None, tile(x1b, t), tile(x1b, t + 1) if t < 3 else None
        )
        if t in (1, 2):
            keep(t, second)
        a = term(t, second)
        for g in range(4):
            for s in range(2):
                a_out[16 * s + slot_of(t, g)] = a[:, 512 * g + 256 * s : 512 * g + 256 * s + 256]
    pl.semaphore_wait(barrier, 46)
    north_of, south_of = lax.rem(l + 1, 32), lax.rem(l + 31, 32)
    send(xb.at[24:32, :], halo.at[0], h_send.at[0], h_recv.at[0], at_lat(north_of), l < 31)
    send(xb.at[0:8, :], halo.at[1], h_send.at[1], h_recv.at[1], at_lat(south_of), l > 0)

    def send_a(s, some):
        for v in some:
            send(a_out.at[16 * s + v], a_in.at[s, w], a_send, a_recv.at[s], at_win(v), w < 15)

    send_a(0, windows)
    send_a(1, windows[:7])
    for s in range(2):
        a_in[s, w] = a_out[16 * s + w]

    @pl.when(l == 0)
    def _():
        halo[0] = jnp.zeros((8, 2048), F32)

    @pl.when(l == 31)
    def _():
        halo[1] = jnp.zeros((8, 2048), F32)

    @pl.when(w == 0)
    def _():
        pb[...] = jnp.zeros(pb.shape, F32)
        p_in[...] = jnp.zeros(p_in.shape, F32)
        ep_in[...] = jnp.zeros(ep_in.shape, F32)

    wait(halo.at[0], h_recv.at[0], l > 0)
    wait(halo.at[1], h_recv.at[1], l < 31)
    low, high = halo[0], halo[1]
    beyond_low = jnp.where(l > 0, advanced(None, low, tile(xb, 0)), 0.0)
    edge = advanced(low, tile(xb, 0), tile(xb, 1))
    x1b[0:8, :] = edge
    bottom = advanced(beyond_low, edge, tile(x1b, 1))
    beyond_high = jnp.where(l < 31, advanced(tile(xb, 3), high, None), 0.0)
    edge = advanced(tile(xb, 2), tile(xb, 3), high)
    x1b[24:32, :] = edge
    top = advanced(tile(x1b, 2), edge, beyond_high)
    keep(0, bottom)
    keep(3, top)
    outer = jnp.where(row < 4, term(0, bottom), term(3, top))
    packed = jnp.where((row8 < 2) | (row8 >= 6), outer[:, :1024], pltpu.roll(outer[:, 1024:], 4, 0))
    holder = lax.rem(y, 2) == xh
    for k in range(8):
        ea_out[k] = packed[:, 128 * k : 128 * k + 128]
    for off in AROUND:
        k = lax.rem(y + off, 8)
        v = lax.rem(k, 2) * 8 + k
        send(ea_out.at[k], ea_in.at[w], ea_send, ea_recv, at_win(v), jnp.logical_and(w < 15, w != v))
    send_a(1, windows[7:])
    ea_in[w] = ea_out[y]
    send_prior(0, w < 15)
    for q in (2, 3):
        send(x2b.at[q], rel.at[q - 2], e_send, rel_recv, at_win(jnp.int32(15)), w == 7)
    send_prior(1, w == 7)

    loads[2].wait()
    loads[3].wait()
    for t in range(4):
        rows = slice(8 * t, 8 * t + 8)
        for g in range(4):
            for q in range(4):
                at = slice(512 * g + 128 * q, 512 * g + 128 * q + 128)
                u = mb[rows, at] + later * xb[rows, at]
                lamb[rows, at] = u
                lb[rows, at] = (
                    kb[0, rows, at].astype(F32) * (ob[0, rows, at] - x1b[rows, at])
                    + kb[1, rows, at].astype(F32) * (ob[1, rows, at] - x2b[q, rows, 128 * g : 128 * g + 128])
                    + u
                )

    def piece(s):
        wait_either(w == 15, a_in.at[s, 0:15], a_in.at[s, 0:14], a_recv.at[s])
        total = jnp.zeros((8, 256), F32)
        for v in range(16):
            p_out[32 * s + v] = total[:, :128]
            p_out[32 * s + 16 + v] = total[:, 128:]
            if v < 15:
                total = total + a_in[s, v]
        for q in (2 * s, 2 * s + 1):
            for v in windows:
                send(p_out.at[16 * q + v], p_in.at[q, w], p_send, p_recv.at[q], at_win(v), v > 0)
            if q > 0:
                send_prior(q, jnp.logical_and(w < 15, w != 7))
        for q in (2 * s, 2 * s + 1):
            p_in[q, w] = p_out[16 * q + w]

    piece(0)

    @pl.when(holder)
    def _():
        wait_either(w == 15, ea_in.at[0:15], ea_in.at[0:14], ea_recv)
        total = jnp.zeros((8, 128), F32)
        for v in range(16):
            ep_out[v] = total
            if v < 15:
                total = total + ea_in[v]
        for v in windows:
            send(ep_out.at[v], ep_in.at[y], ep_send, ep_recv, at_win(v), v > 0)
        ep_in[y] = ep_out[w]

    piece(1)
    pl.when(w == 15)(relay_prior)

    for load in loads[4:]:
        load.wait()
    lsf[...] = gathered(ls[...], 32, 32) * 2.0**-22
    lnf[...] = gathered(lo[...], 16, 128)
    save_scale = pltpu.make_async_copy(lnf, lon_scale, out_sem.at[0])
    save_scale.start()

    @pl.when(w > 0)
    def _():
        wait_either(holder, ep_in.at[0:7], ep_in.at[0:8], ep_recv)

    for q in range(4):
        wait(p_in.at[q, 0:15], p_recv.at[q], w > 0)
        wait(pb.at[q], e_recv.at[q], w > 0)
        for g in range(4):
            at = slice(512 * g + 128 * q, 512 * g + 128 * q + 128)
            outer = ep_in[4 * (g % 2) + q]
            if g >= 2:
                outer = pltpu.roll(outer, 4, 0)
            for t in range(4):
                rows = slice(8 * t, 8 * t + 8)
                prior = 0.5 * pb[q, rows, 128 * g : 128 * g + 128]
                lamb[rows, at] = lamb[rows, at] - prior
                earlier = p_in[q, slot_of(t, g)]
                if t == 0:
                    earlier = jnp.where(row1 < 2, outer, earlier)
                if t == 3:
                    earlier = jnp.where(row1 >= 6, outer, earlier)
                rb[32 * g + 8 * t : 32 * g + 8 * t + 8, :] = lb[rows, at] - prior - (earlier + prior) * inv
        tb[q] = rb[...].T
        for off in AROUND:
            to = lax.rem(z + off, 8)
            target = to * 4 + q
            when = None if off else (group != q)
            send(tb.at[q, pl.ds(pl.multiple_of(to * 16, 16), 16), :], zb.at[l], z_send, z_recv, at_lat(target), when)
    here = pl.ds(pl.multiple_of(z * 16, 16), 16)
    zb[l] = tb[group, here, :]
    save = pltpu.make_async_copy(lamb, new_mult, out_sem.at[1])
    save.start()

    wait(zb.at[0:31], z_recv)

    def sink(j, h, value):
        ob2[j, 8 * h : 8 * h + 8, :] = value

    operator(
        lambda j, h: zb[j, 8 * h : 8 * h + 8, :], sink, 32, 16, rows_of(twb, 0, 32), rows_of(twb, 32, 32), lsf, uv, wfb, wbb
    )
    for m in bands:
        send(ob2.at[m], turned.at[group, here, :], y_send, y_recv, at_lat(m))
    own = pltpu.make_async_copy(ob2.at[l], turned.at[group, here, :], out_sem.at[2])
    own.start()

    wait(halo.at[0], h_send.at[0], l < 31)
    wait(halo.at[1], h_send.at[1], l > 0)

    @pl.when(w < 15)
    def _():
        wait(a_out.at[0:30], a_send)
        wait(x2b, e_send)
        wait_either(holder, ea_out.at[0:7], ea_out.at[0:8], ea_send)

    wait_either(w == 0, p_out.at[0:60], p_out.at[0:56], p_send)

    @pl.when(holder)
    def _():
        wait_either(w == 0, ep_out.at[0:15], ep_out.at[0:14], ep_send)

    wait(rel, rel_send, w == 15)
    wait(zb.at[0:31], z_send)
    save_scale.wait()
    save.wait()
    own.wait()
    wait(ob2.at[0:31], y_send)
    wait(ob2.at[0:31], y_recv)


def longitude_kernel(
    state, lam, turned, lon_scale, tw, wf, wb,
    new_state, new_mult,
    xb, lamb, yb, lnf, twb, wfb, wbb, vb, uv, outb, in_sem, out_sem,
):
    loads = [
        pltpu.make_async_copy(src, dst, in_sem.at[i])
        for i, (src, dst) in enumerate(
            [(turned, yb), (tw, twb), (wf, wfb), (lon_scale, lnf), (wb, wbb), (state, xb), (lam, lamb)]
        )
    ]
    for load in loads:
        load.start()
    loads[0].wait()
    loads[1].wait()
    for q in range(4):
        flat = yb[q].T
        for g in range(4):
            vb[4 * g + q] = flat[32 * g : 32 * g + 32, :]
    for load in loads[2:]:
        load.wait()
    save = pltpu.make_async_copy(lamb, new_mult, out_sem.at[0])
    save.start()

    def sink(j, h, value):
        rows, columns = slice(8 * h, 8 * h + 8), slice(128 * j, 128 * j + 128)
        outb[rows, columns] = xb[rows, columns] + value

    operator(lambda j, h: vb[j, 8 * h : 8 * h + 8, :], sink, 16, 32, rows_of(twb, 0, 16), rows_of(twb, 16, 16), lnf, uv, wfb, wbb)
    result = pltpu.make_async_copy(outb, new_state, out_sem.at[1])
    result.start()
    save.wait()
    result.wait()


def per_device(state, multipliers, observations, obs_mask, speed, drift, kappa, lat_spectrum, lon_spectrum):
    band, nlon = state.shape[2:]
    (tw_lat, w_lat), (tw_lon, w_lon) = tables(32, 32), tables(16, 128)
    hbm = pl.BlockSpec(memory_space=pltpu.HBM)
    vmem = pltpu.VMEM
    dma = pltpu.SemaphoreType.DMA
    grid = jax.ShapeDtypeStruct((band, nlon), F32)
    field = vmem((32, 2048), F32)
    turned, lam, lon_scale = pl.pallas_call(
        exchange_kernel,
        out_shape=[jax.ShapeDtypeStruct((4, 128, 128), F32), grid, jax.ShapeDtypeStruct((16, 128), F32)],
        in_specs=[hbm] * 4 + [pl.BlockSpec(memory_space=pltpu.SMEM)] * 3 + [hbm] * 5,
        out_specs=[hbm] * 3,
        scratch_shapes=[
            field, field, vmem((2, 32, 2048), F32), vmem((2, 32, 2048), jnp.int32),
            vmem((1, 1024), F32), vmem((1, 2048), F32), vmem((64, 128), F32), vmem((2, 256, 128), BF16), vmem((2, 128, 256), BF16),
            vmem((2, 8, 2048), F32), field, vmem((4, 32, 512), F32), vmem((4, 32, 512), F32), field, field,
            vmem((32, 8, 256), F32), vmem((2, 16, 8, 256), F32), vmem((64, 8, 128), F32), vmem((4, 16, 8, 128), F32),
            vmem((8, 8, 128), F32), vmem((16, 8, 128), F32), vmem((16, 8, 128), F32), vmem((8, 8, 128), F32), vmem((2, 32, 512), F32),
            vmem((128, 128), F32), vmem((4, 128, 128), F32), vmem((32, 16, 128), F32), vmem((32, 16, 128), F32),
            vmem((512, 256), F32), vmem((32, 128), F32), vmem((16, 128), F32),
            dma((9,)), dma((3,)), dma((2,)), dma((2,)), dma, dma((2,)), dma, dma((4,)),
            dma, dma, dma, dma, dma, dma((4,)), dma, dma, dma, dma, dma, dma,
        ],
        compiler_params=pltpu.CompilerParams(collective_id=0, has_side_effects=True, vmem_limit_bytes=67043328),
        name="exchange",
    )(
        state[0, 0], multipliers[0, 0], observations[0, :, 0], obs_mask[0], speed, drift, kappa, lat_spectrum, lon_spectrum,
        jnp.asarray(tw_lat), jnp.asarray(halves(w_lat)), jnp.asarray(halves(np.ascontiguousarray(w_lat.T))),
    )
    new_state, new_mult = pl.pallas_call(
        longitude_kernel,
        out_shape=[grid] * 2,
        in_specs=[hbm] * 7,
        out_specs=[hbm] * 2,
        scratch_shapes=[
            field, field, vmem((4, 128, 128), F32), vmem((16, 128), F32), vmem((32, 128), F32),
            vmem((2, 256, 128), BF16), vmem((2, 128, 256), BF16), vmem((16, 32, 128), F32), vmem((512, 256), F32), field,
            dma((7,)), dma((2,)),
        ],
        compiler_params=pltpu.CompilerParams(vmem_limit_bytes=67043328),
        name="longitudes",
    )(
        state[0, 0], lam, turned, lon_scale,
        jnp.asarray(tw_lon), jnp.asarray(halves(w_lon)), jnp.asarray(halves(np.ascontiguousarray(w_lon.T))),
    )
    return new_state[None, None], new_mult[None, None]


def solution(mesh):
    finer = Mesh(mesh.devices.reshape(2, 8, 8, 2, 2), AXES)
    placed = (
        P(WIN, None, LAT, None),
        P(WIN, None, LAT, None),
        P(WIN, None, None, LAT, None),
        P(WIN, None, LAT, None),
        P(),
        P(),
        P(),
        P(),
        P(),
    )
    return jax.shard_map(
        per_device,
        mesh=finer,
        in_specs=placed,
        out_specs=(P(WIN, None, LAT, None), P(WIN, None, LAT, None)),
        check_vma=False,
    )
```

time: 67.6 us -> 55.3 us (0.82)
  the two profiles are of different devices: /device:TPU:9 before, /device:TPU:6 now
where the time goes in v2:
time: 55.3 us; the launch traced here: 54.4 us
  Pallas kernels  51.8 us (94%)
  between operations  2.58 us (5%)
    pallas_call x1, Pallas kernels, per_device(): pl.pallas_call(exchange_kernel, out_shape=[jax.ShapeDtypeStruct((4, 128,...  49 us
    pallas_call x1, Pallas kernels, per_device(): pl.pallas_call(longitude_kernel, out_shape=[grid] * 2, in_specs=[hbm] * 7...  2.83 us

profile of v2, /device:TPU:6, one launch (start us, length us, event | category | flops | bytes accessed | tf_op | source)
XLA Modules:
  0.0 54.4 jit_solution(4212820528349400461)
XLA Ops:
  2.6 49.0 %exchange.1 = (f32[4,128,128]{2,1,0:T(8,128)}, f32[32,2048]{1,0:T(8,128)}, f32[16,128]{1,0:T(8,128)}) custom-call(f32[32,2048]{1,0:T(8,128)} %bitcast.6, f32[32,2048]{1,0:T(8,128)} %bitcast.10, f32[2,32,2048]{2,1,0:T(8,128)} %bitcast.8, s32[2,32,2048]{2,1,0:T(8,128)} %bitcast.9, f32[1]{0:T(128)S(6)} %copy.17.speed, f32[1]{0:T(128)S(6)} %copy.18.drift, ...), custom_call_target="tpu_custom_call" | custom-call | tf_op jit(solution)/shard_map/exchange/pallas_call | solution.py:541
  51.6 2.8 %longitudes.1 = (f32[32,2048]{1,0:T(8,128)}, f32[32,2048]{1,0:T(8,128)}) custom-call(f32[32,2048]{1,0:T(8,128)} %bitcast.7, f32[32,2048]{1,0:T(8,128)} %get-tuple-element.7.lam, f32[4,128,128]{2,1,0:T(8,128)} %get-tuple-element.8.turned, f32[16,128]{1,0:T(8,128)} %get-tuple-element.9.lon_scale, f32[32,128]{1,0:T(8,128)} %constant.15.clone.tw, ...), custom_call_target="tpu_custom_call" | custom-call | tf_op jit(solution)/shard_map/longitudes/pallas_call | solution.py:563

commit v3 on v2

--- a/solution.py
+++ b/solution.py
@@ -17,6 +17,7 @@
 BF16 = jnp.bfloat16
 AROUND = (4, 5, 3, 6, 2, 7, 1, 0)
 TILE_OF = (1, 0, 2, 3)
+PARTS = 4
 
 
 def rotated(c, s, angle):
@@ -132,19 +133,21 @@
     return np.concatenate([cos, sin], 0).astype(np.float32), full.astype(np.float32)
 
 
-def halves(full):
+def weights(full):
     import ml_dtypes
 
-    hi = full.astype(ml_dtypes.bfloat16)
-    lo = (full - hi.astype(np.float32)).astype(ml_dtypes.bfloat16)
-    return np.stack([hi, lo])
-
-
-def dot3(a, hi, lo):
-    a_hi = a.astype(BF16)
-    a_lo = (a - a_hi.astype(F32)).astype(BF16)
-    dot = functools.partial(jnp.dot, preferred_element_type=F32)
-    return dot(a_hi, hi) + (dot(a_lo, hi) + dot(a_hi, lo))
+    first = full.astype(ml_dtypes.bfloat16)
+    rest = (full - first.astype(np.float32)).astype(ml_dtypes.bfloat16)
+    return np.concatenate([first, rest], 1), np.ascontiguousarray(np.concatenate([first.T, first.T, rest.T], 0))
+
+
+def parted(a):
+    first = a.astype(BF16)
+    return first, (a - first.astype(F32)).astype(BF16)
+
+
+def dot(a, b):
+    return jnp.dot(a, b, preferred_element_type=F32)
 
 
 def gathered(spec, n1, n2):
@@ -159,7 +162,6 @@
     place = lax.broadcasted_iota(jnp.int32, (n, 128), 0) >> (n1.bit_length() - 1)
     lane = lax.broadcasted_iota(jnp.int32, (n, 128), 1) & (n2 - 1)
     pick = jnp.where(place == lane, 1.0, 0.0).astype(BF16)
-    dot = functools.partial(jnp.dot, preferred_element_type=F32)
     return dot(first, pick) + dot(second, pick) + dot(third, pick)
 
 
@@ -174,13 +176,18 @@
             at = depth * k + 8 * h
             uv[at : at + 8, 0:128] = u[k]
             uv[at : at + 8, 128:256] = v[k]
-    for q in range(4):
-        rows = slice(128 * q, 128 * q + 128)
+    count = 512 // PARTS
+    for q in range(PARTS):
+        rows = slice(count * q, count * (q + 1))
         factor = jnp.concatenate(
-            [jnp.broadcast_to(scale[k : k + 1, :], (depth, 128)) for k in range(128 * q // depth, 128 * (q + 1) // depth)], axis=0
+            [jnp.broadcast_to(scale[k : k + 1, :], (depth, 128)) for k in range(count * q // depth, count * (q + 1) // depth)],
+            axis=0,
         )
-        spectral = dot3(uv[rows, :], wf[0], wf[1]) * factor
-        uv[rows, :] = dot3(spectral, wb[0], wb[1])
+        first, rest = parted(uv[rows, :])
+        both = dot(first, wf[...])
+        spectral = (both[:, :128] + (both[:, 128:] + dot(rest, wf[:, 0:128]))) * factor
+        first, rest = parted(spectral)
+        uv[rows, :] = dot(jnp.concatenate([first, rest], axis=1), wb[0:256, :]) + dot(first, wb[256:384, :])
     for h in range(depth // 8):
         at = [depth * k + 8 * h for k in range(n1)]
         out = synthesise([uv[a : a + 8, 0:128] for a in at], [uv[a : a + 8, 128:256] for a in at], cos, sin)
@@ -221,13 +228,21 @@
     for load in loads:
         load.start()
 
-    windows = [lax.rem(xh + far, 2) * 8 + lax.rem(y + off, 8) for off in AROUND for far in (1, 0) if off or far]
-    bands = [lax.rem(z + off, 8) * 4 + lax.rem(group + near, 4) for off in AROUND for near in (2, 3, 1, 0) if off or near]
+    def ahead(place, off):
+        return jnp.where(place + off >= 8, place + off - 8, place + off) if off else place
+
+    windows, bands = [], []
+    for off in AROUND:
+        yy, zz = ahead(y, off), ahead(z, off)
+        for xx in (1 - xh, xh):
+            if off or xx is not xh:
+                windows.append((xx * 8 + yy, (xx, yy, z, xl, core)))
+        for xx, cc in ((1 - xl, core), (1 - xl, 1 - core), (xl, 1 - core), (xl, core)):
+            if off or xx is not xl or cc is not core:
+                bands.append((zz * 4 + xx * 2 + cc, (xh, y, zz, xx, cc)))
     barrier = pltpu.get_barrier_semaphore()
-    for v in windows:
-        pl.semaphore_signal(barrier, inc=1, device_id=at_win(v), device_id_type=pl.DeviceIdType.MESH)
-    for m in bands:
-        pl.semaphore_signal(barrier, inc=1, device_id=at_lat(m), device_id_type=pl.DeviceIdType.MESH)
+    for _, device in windows + bands:
+        pl.semaphore_signal(barrier, inc=1, device_id=device, device_id_type=pl.DeviceIdType.MESH)
 
     def guarded(when, act):
         if when is None:
@@ -319,8 +334,8 @@
     send(xb.at[0:8, :], halo.at[1], h_send.at[1], h_recv.at[1], at_lat(south_of), l > 0)
 
     def send_a(s, some):
-        for v in some:
-            send(a_out.at[16 * s + v], a_in.at[s, w], a_send, a_recv.at[s], at_win(v), w < 15)
+        for v, device in some:
+            send(a_out.at[16 * s + v], a_in.at[s, w], a_send, a_recv.at[s], device, w < 15)
 
     send_a(0, windows)
     send_a(1, windows[:7])
@@ -360,9 +375,10 @@
     for k in range(8):
         ea_out[k] = packed[:, 128 * k : 128 * k + 128]
     for off in AROUND:
-        k = lax.rem(y + off, 8)
-        v = lax.rem(k, 2) * 8 + k
-        send(ea_out.at[k], ea_in.at[w], ea_send, ea_recv, at_win(v), jnp.logical_and(w < 15, w != v))
+        k = ahead(y, off)
+        row_of = lax.rem(k, 2)
+        v = row_of * 8 + k
+        send(ea_out.at[k], ea_in.at[w], ea_send, ea_recv, (row_of, k, z, xl, core), jnp.logical_and(w < 15, w != v))
     send_a(1, windows[7:])
     ea_in[w] = ea_out[y]
     send_prior(0, w < 15)
@@ -394,8 +410,8 @@
             if v < 15:
                 total = total + a_in[s, v]
         for q in (2 * s, 2 * s + 1):
-            for v in windows:
-                send(p_out.at[16 * q + v], p_in.at[q, w], p_send, p_recv.at[q], at_win(v), v > 0)
+            for v, device in windows:
+                send(p_out.at[16 * q + v], p_in.at[q, w], p_send, p_recv.at[q], device, v > 0)
             if q > 0:
                 send_prior(q, jnp.logical_and(w < 15, w != 7))
         for q in (2 * s, 2 * s + 1):
@@ -411,8 +427,8 @@
             ep_out[v] = total
             if v < 15:
                 total = total + ea_in[v]
-        for v in windows:
-            send(ep_out.at[v], ep_in.at[y], ep_send, ep_recv, at_win(v), v > 0)
+        for v, device in windows:
+            send(ep_out.at[v], ep_in.at[y], ep_send, ep_recv, device, v > 0)
         ep_in[y] = ep_out[w]
 
     piece(1)
@@ -449,10 +465,10 @@
                 rb[32 * g + 8 * t : 32 * g + 8 * t + 8, :] = lb[rows, at] - prior - (earlier + prior) * inv
         tb[q] = rb[...].T
         for off in AROUND:
-            to = lax.rem(z + off, 8)
-            target = to * 4 + q
+            to = ahead(z, off)
             when = None if off else (group != q)
-            send(tb.at[q, pl.ds(pl.multiple_of(to * 16, 16), 16), :], zb.at[l], z_send, z_recv, at_lat(target), when)
+            device = (xh, y, to, jnp.int32(q // 2), jnp.int32(q % 2))
+            send(tb.at[q, pl.ds(pl.multiple_of(to * 16, 16), 16), :], zb.at[l], z_send, z_recv, device, when)
     here = pl.ds(pl.multiple_of(z * 16, 16), 16)
     zb[l] = tb[group, here, :]
     save = pltpu.make_async_copy(lamb, new_mult, out_sem.at[1])
@@ -466,8 +482,8 @@
     operator(
         lambda j, h: zb[j, 8 * h : 8 * h + 8, :], sink, 32, 16, rows_of(twb, 0, 32), rows_of(twb, 32, 32), lsf, uv, wfb, wbb
     )
-    for m in bands:
-        send(ob2.at[m], turned.at[group, here, :], y_send, y_recv, at_lat(m))
+    for m, device in bands:
+        send(ob2.at[m], turned.at[group, here, :], y_send, y_recv, device)
     own = pltpu.make_async_copy(ob2.at[l], turned.at[group, here, :], out_sem.at[2])
     own.start()
 
@@ -514,20 +530,27 @@
         flat = yb[q].T
         for g in range(4):
             vb[4 * g + q] = flat[32 * g : 32 * g + 32, :]
-    for load in loads[2:]:
+    for load in loads[2:5]:
         load.wait()
-    save = pltpu.make_async_copy(lamb, new_mult, out_sem.at[0])
-    save.start()
+    save = pltpu.make_async_copy(lamb, new_mult, out_sem.at[4])
+    results = [
+        pltpu.make_async_copy(outb.at[8 * h : 8 * h + 8, :], new_state.at[8 * h : 8 * h + 8, :], out_sem.at[h]) for h in range(4)
+    ]
 
     def sink(j, h, value):
+        if (j, h) == (0, 0):
+            loads[5].wait()
+            loads[6].wait()
+            save.start()
         rows, columns = slice(8 * h, 8 * h + 8), slice(128 * j, 128 * j + 128)
         outb[rows, columns] = xb[rows, columns] + value
+        if j == 15:
+            results[h].start()
 
     operator(lambda j, h: vb[j, 8 * h : 8 * h + 8, :], sink, 16, 32, rows_of(twb, 0, 16), rows_of(twb, 16, 16), lnf, uv, wfb, wbb)
-    result = pltpu.make_async_copy(outb, new_state, out_sem.at[1])
-    result.start()
     save.wait()
-    result.wait()
+    for result in results:
+        result.wait()
 
 
 def per_device(state, multipliers, observations, obs_mask, speed, drift, kappa, lat_spectrum, lon_spectrum):
@@ -545,7 +568,7 @@
         out_specs=[hbm] * 3,
         scratch_shapes=[
             field, field, vmem((2, 32, 2048), F32), vmem((2, 32, 2048), jnp.int32),
-            vmem((1, 1024), F32), vmem((1, 2048), F32), vmem((64, 128), F32), vmem((2, 256, 128), BF16), vmem((2, 128, 256), BF16),
+            vmem((1, 1024), F32), vmem((1, 2048), F32), vmem((64, 128), F32), vmem((256, 256), BF16), vmem((384, 256), BF16),
             vmem((2, 8, 2048), F32), field, vmem((4, 32, 512), F32), vmem((4, 32, 512), F32), field, field,
             vmem((32, 8, 256), F32), vmem((2, 16, 8, 256), F32), vmem((64, 8, 128), F32), vmem((4, 16, 8, 128), F32),
             vmem((8, 8, 128), F32), vmem((16, 8, 128), F32), vmem((16, 8, 128), F32), vmem((8, 8, 128), F32), vmem((2, 32, 512), F32),
@@ -558,7 +581,7 @@
         name="exchange",
     )(
         state[0, 0], multipliers[0, 0], observations[0, :, 0], obs_mask[0], speed, drift, kappa, lat_spectrum, lon_spectrum,
-        jnp.asarray(tw_lat), jnp.asarray(halves(w_lat)), jnp.asarray(halves(np.ascontiguousarray(w_lat.T))),
+        jnp.asarray(tw_lat), *(jnp.asarray(part) for part in weights(w_lat)),
     )
     new_state, new_mult = pl.pallas_call(
         longitude_kernel,
@@ -567,14 +590,14 @@
         out_specs=[hbm] * 2,
         scratch_shapes=[
             field, field, vmem((4, 128, 128), F32), vmem((16, 128), F32), vmem((32, 128), F32),
-            vmem((2, 256, 128), BF16), vmem((2, 128, 256), BF16), vmem((16, 32, 128), F32), vmem((512, 256), F32), field,
-            dma((7,)), dma((2,)),
+            vmem((256, 256), BF16), vmem((384, 256), BF16), vmem((16, 32, 128), F32), vmem((512, 256), F32), field,
+            dma((7,)), dma((5,)),
         ],
         compiler_params=pltpu.CompilerParams(vmem_limit_bytes=67043328),
         name="longitudes",
     )(
         state[0, 0], lam, turned, lon_scale,
-        jnp.asarray(tw_lon), jnp.asarray(halves(w_lon)), jnp.asarray(halves(np.ascontiguousarray(w_lon.T))),
+        jnp.asarray(tw_lon), *(jnp.asarray(part) for part in weights(w_lon)),
     )
     return new_state[None, None], new_mult[None, None]
 

time: 55.3 us -> 54.2 us (0.980)
  Pallas kernels: 51.8 us -> 50.9 us
    pallas_call x1, Pallas kernels: 49 us -> 48.4 us  [per_device(): pl.pallas_call(exchange_kernel, out_shape=[jax.ShapeDtypeStruct((4, 128,...]
where the time goes in v3:
time: 54.2 us; the launch traced here: 53.5 us
  Pallas kernels  50.9 us (94%)
  between operations  2.58 us (5%)
    pallas_call x1, Pallas kernels, per_device(): pl.pallas_call(exchange_kernel, out_shape=[jax.ShapeDtypeStruct((4, 128,...  48.4 us
    pallas_call x1, Pallas kernels, per_device(): pl.pallas_call(longitude_kernel, out_shape=[grid] * 2, in_specs=[hbm] * 7...  2.53 us

profile of v3, /device:TPU:6, one launch (start us, length us, event | category | flops | bytes accessed | tf_op | source)
XLA Modules:
  0.0 53.5 jit_solution(9169828540746588403)
XLA Ops:
  2.6 48.4 %exchange.1 = (f32[4,128,128]{2,1,0:T(8,128)}, f32[32,2048]{1,0:T(8,128)}, f32[16,128]{1,0:T(8,128)}) custom-call(f32[32,2048]{1,0:T(8,128)} %bitcast.6, f32[32,2048]{1,0:T(8,128)} %bitcast.10, f32[2,32,2048]{2,1,0:T(8,128)} %bitcast.8, s32[2,32,2048]{2,1,0:T(8,128)} %bitcast.9, f32[1]{0:T(128)S(6)} %copy.17.speed, f32[1]{0:T(128)S(6)} %copy.18.drift, ...), custom_call_target="tpu_custom_call" | custom-call | tf_op jit(solution)/shard_map/exchange/pallas_call | solution.py:564
  50.9 2.5 %longitudes.1 = (f32[32,2048]{1,0:T(8,128)}, f32[32,2048]{1,0:T(8,128)}) custom-call(f32[32,2048]{1,0:T(8,128)} %bitcast.7, f32[32,2048]{1,0:T(8,128)} %get-tuple-element.7.lam, f32[4,128,128]{2,1,0:T(8,128)} %get-tuple-element.8.turned, f32[16,128]{1,0:T(8,128)} %get-tuple-element.9.lon_scale, f32[32,128]{1,0:T(8,128)} %constant.15.clone.tw, ...), custom_call_target="tpu_custom_call" | custom-call | tf_op jit(solution)/shard_map/longitudes/pallas_call | solution.py:586

commit v4 on v3

--- a/solution.py
+++ b/solution.py
@@ -17,7 +17,7 @@
 BF16 = jnp.bfloat16
 AROUND = (4, 5, 3, 6, 2, 7, 1, 0)
 TILE_OF = (1, 0, 2, 3)
-PARTS = 4
+PARTS = 2
 
 
 def rotated(c, s, angle):
@@ -203,7 +203,7 @@
     state, mult, obs, mask, speed, drift, kappa, lat_spec, lon_spec, tw, wf, wb,
     turned, new_mult, lon_scale,
     xb, mb, ob, kb, ls, lo, twb, wfb, wbb,
-    halo, x1b, x2b, pb, lb, lamb, a_out, a_in, p_out, p_in, ea_out, ea_in, ep_out, ep_in, rel,
+    halo, x1b, x2b, pb, lb, lamb, a_out, a_in, p0_out, p0_in, p_out, p_in, ea_out, ea_in, ep_out, ep_in, rel,
     rb, tb, zb, ob2, uv, lsf, lnf,
     in_sem, out_sem, h_send, h_recv, a_send, a_recv, p_send, p_recv, ea_send, ea_recv, ep_send, ep_recv,
     e_send, e_recv, rel_send, rel_recv, z_send, z_recv, y_send, y_recv,
@@ -353,6 +353,7 @@
     @pl.when(w == 0)
     def _():
         pb[...] = jnp.zeros(pb.shape, F32)
+        p0_in[...] = jnp.zeros(p0_in.shape, F32)
         p_in[...] = jnp.zeros(p_in.shape, F32)
         ep_in[...] = jnp.zeros(ep_in.shape, F32)
 
@@ -405,16 +406,24 @@
         wait_either(w == 15, a_in.at[s, 0:15], a_in.at[s, 0:14], a_recv.at[s])
         total = jnp.zeros((8, 256), F32)
         for v in range(16):
-            p_out[32 * s + v] = total[:, :128]
-            p_out[32 * s + 16 + v] = total[:, 128:]
+            if s == 0:
+                p0_out[v] = total
+            else:
+                p_out[v] = total[:, :128]
+                p_out[16 + v] = total[:, 128:]
             if v < 15:
                 total = total + a_in[s, v]
-        for q in (2 * s, 2 * s + 1):
+        if s == 0:
             for v, device in windows:
-                send(p_out.at[16 * q + v], p_in.at[q, w], p_send, p_recv.at[q], device, v > 0)
-            if q > 0:
-                send_prior(q, jnp.logical_and(w < 15, w != 7))
-        for q in (2 * s, 2 * s + 1):
+                send(p0_out.at[v], p0_in.at[w], p_send, p_recv.at[0], device, v > 0)
+            send_prior(1, jnp.logical_and(w < 15, w != 7))
+            p0_in[w] = p0_out[w]
+            return
+        for q in range(2):
+            for v, device in windows:
+                send(p_out.at[16 * q + v], p_in.at[q, w], p_send, p_recv.at[1 + q], device, v > 0)
+            send_prior(2 + q, jnp.logical_and(w < 15, w != 7))
+        for q in range(2):
             p_in[q, w] = p_out[16 * q + w]
 
     piece(0)
@@ -446,7 +455,10 @@
         wait_either(holder, ep_in.at[0:7], ep_in.at[0:8], ep_recv)
 
     for q in range(4):
-        wait(p_in.at[q, 0:15], p_recv.at[q], w > 0)
+        if q == 0:
+            wait(p0_in.at[0:15], p_recv.at[0], w > 0)
+        if q >= 2:
+            wait(p_in.at[q - 2, 0:15], p_recv.at[q - 1], w > 0)
         wait(pb.at[q], e_recv.at[q], w > 0)
         for g in range(4):
             at = slice(512 * g + 128 * q, 512 * g + 128 * q + 128)
@@ -457,7 +469,10 @@
                 rows = slice(8 * t, 8 * t + 8)
                 prior = 0.5 * pb[q, rows, 128 * g : 128 * g + 128]
                 lamb[rows, at] = lamb[rows, at] - prior
-                earlier = p_in[q, slot_of(t, g)]
+                if q < 2:
+                    earlier = p0_in[slot_of(t, g), :, 128 * q : 128 * q + 128]
+                else:
+                    earlier = p_in[q - 2, slot_of(t, g)]
                 if t == 0:
                     earlier = jnp.where(row1 < 2, outer, earlier)
                 if t == 3:
@@ -496,7 +511,7 @@
         wait(x2b, e_send)
         wait_either(holder, ea_out.at[0:7], ea_out.at[0:8], ea_send)
 
-    wait_either(w == 0, p_out.at[0:60], p_out.at[0:56], p_send)
+    wait_either(w == 0, a_out.at[0:30], a_out.at[0:28], p_send)
 
     @pl.when(holder)
     def _():
@@ -570,11 +585,12 @@
             field, field, vmem((2, 32, 2048), F32), vmem((2, 32, 2048), jnp.int32),
             vmem((1, 1024), F32), vmem((1, 2048), F32), vmem((64, 128), F32), vmem((256, 256), BF16), vmem((384, 256), BF16),
             vmem((2, 8, 2048), F32), field, vmem((4, 32, 512), F32), vmem((4, 32, 512), F32), field, field,
-            vmem((32, 8, 256), F32), vmem((2, 16, 8, 256), F32), vmem((64, 8, 128), F32), vmem((4, 16, 8, 128), F32),
+            vmem((32, 8, 256), F32), vmem((2, 16, 8, 256), F32), vmem((16, 8, 256), F32), vmem((16, 8, 256), F32),
+            vmem((32, 8, 128), F32), vmem((2, 16, 8, 128), F32),
             vmem((8, 8, 128), F32), vmem((16, 8, 128), F32), vmem((16, 8, 128), F32), vmem((8, 8, 128), F32), vmem((2, 32, 512), F32),
             vmem((128, 128), F32), vmem((4, 128, 128), F32), vmem((32, 16, 128), F32), vmem((32, 16, 128), F32),
             vmem((512, 256), F32), vmem((32, 128), F32), vmem((16, 128), F32),
-            dma((9,)), dma((3,)), dma((2,)), dma((2,)), dma, dma((2,)), dma, dma((4,)),
+            dma((9,)), dma((3,)), dma((2,)), dma((2,)), dma, dma((2,)), dma, dma((3,)),
             dma, dma, dma, dma, dma, dma((4,)), dma, dma, dma, dma, dma, dma,
         ],
         compiler_params=pltpu.CompilerParams(collective_id=0, has_side_effects=True, vmem_limit_bytes=67043328),

time: 54.2 us -> 54.2 us (level)
  no operation moved by 1% of the time
where the time goes in v4:
time: 54.2 us; the launch traced here: 53.6 us
  Pallas kernels  51 us (94%)
  between operations  2.58 us (5%)
    pallas_call x1, Pallas kernels, per_device(): pl.pallas_call(exchange_kernel, out_shape=[jax.ShapeDtypeStruct((4, 128,...  48.5 us
    pallas_call x1, Pallas kernels, per_device(): pl.pallas_call(longitude_kernel, out_shape=[grid] * 2, in_specs=[hbm] * 7...  2.5 us

profile of v4, /device:TPU:6, one launch (start us, length us, event | category | flops | bytes accessed | tf_op | source)
XLA Modules:
  0.0 53.6 jit_solution(14987389931417223671)
XLA Ops:
  2.6 48.5 %exchange.1 = (f32[4,128,128]{2,1,0:T(8,128)}, f32[32,2048]{1,0:T(8,128)}, f32[16,128]{1,0:T(8,128)}) custom-call(f32[32,2048]{1,0:T(8,128)} %bitcast.6, f32[32,2048]{1,0:T(8,128)} %bitcast.10, f32[2,32,2048]{2,1,0:T(8,128)} %bitcast.8, s32[2,32,2048]{2,1,0:T(8,128)} %bitcast.9, f32[1]{0:T(128)S(6)} %copy.17.speed, f32[1]{0:T(128)S(6)} %copy.18.drift, ...), custom_call_target="tpu_custom_call" | custom-call | tf_op jit(solution)/shard_map/exchange/pallas_call | solution.py:579
  51.0 2.5 %longitudes.1 = (f32[32,2048]{1,0:T(8,128)}, f32[32,2048]{1,0:T(8,128)}) custom-call(f32[32,2048]{1,0:T(8,128)} %bitcast.7, f32[32,2048]{1,0:T(8,128)} %get-tuple-element.7.lam, f32[4,128,128]{2,1,0:T(8,128)} %get-tuple-element.8.turned, f32[16,128]{1,0:T(8,128)} %get-tuple-element.9.lon_scale, f32[32,128]{1,0:T(8,128)} %constant.15.clone.tw, ...), custom_call_target="tpu_custom_call" | custom-call | tf_op jit(solution)/shard_map/longitudes/pallas_call | solution.py:602

commit v5 on v3

--- a/solution.py
+++ b/solution.py
@@ -412,7 +412,10 @@
         for q in (2 * s, 2 * s + 1):
             for v, device in windows:
                 send(p_out.at[16 * q + v], p_in.at[q, w], p_send, p_recv.at[q], device, v > 0)
-            if q > 0:
+            if q == 1:
+                send_prior(q, jnp.logical_and(w < 15, w != 7))
+        if s == 1:
+            for q in (2, 3):
                 send_prior(q, jnp.logical_and(w < 15, w != 7))
         for q in (2 * s, 2 * s + 1):
             p_in[q, w] = p_out[16 * q + w]

time: 54.2 us -> 54.4 us (level)
  no operation moved by 1% of the time
where the time goes in v5:
time: 54.4 us; the launch traced here: 53.4 us
  Pallas kernels  50.8 us (93%)
  between operations  2.58 us (5%)
    pallas_call x1, Pallas kernels, per_device(): pl.pallas_call(exchange_kernel, out_shape=[jax.ShapeDtypeStruct((4, 128,...  48.3 us
    pallas_call x1, Pallas kernels, per_device(): pl.pallas_call(longitude_kernel, out_shape=[grid] * 2, in_specs=[hbm] * 7...  2.53 us

profile of v5, /device:TPU:6, one launch (start us, length us, event | category | flops | bytes accessed | tf_op | source)
XLA Modules:
  0.0 53.4 jit_solution(18262078255494404865)
XLA Ops:
  2.6 48.3 %exchange.1 = (f32[4,128,128]{2,1,0:T(8,128)}, f32[32,2048]{1,0:T(8,128)}, f32[16,128]{1,0:T(8,128)}) custom-call(f32[32,2048]{1,0:T(8,128)} %bitcast.6, f32[32,2048]{1,0:T(8,128)} %bitcast.10, f32[2,32,2048]{2,1,0:T(8,128)} %bitcast.8, s32[2,32,2048]{2,1,0:T(8,128)} %bitcast.9, f32[1]{0:T(128)S(6)} %copy.17.speed, f32[1]{0:T(128)S(6)} %copy.18.drift, ...), custom_call_target="tpu_custom_call" | custom-call | tf_op jit(solution)/shard_map/exchange/pallas_call | solution.py:567
  50.8 2.5 %longitudes.1 = (f32[32,2048]{1,0:T(8,128)}, f32[32,2048]{1,0:T(8,128)}) custom-call(f32[32,2048]{1,0:T(8,128)} %bitcast.7, f32[32,2048]{1,0:T(8,128)} %get-tuple-element.7.lam, f32[4,128,128]{2,1,0:T(8,128)} %get-tuple-element.8.turned, f32[16,128]{1,0:T(8,128)} %get-tuple-element.9.lon_scale, f32[32,128]{1,0:T(8,128)} %constant.15.clone.tw, ...), custom_call_target="tpu_custom_call" | custom-call | tf_op jit(solution)/shard_map/longitudes/pallas_call | solution.py:589
